TPU v7x, 32 devices: a whole 2x2x4 slice. The times are simulated.
32 devices in a mesh: gx: 4 (over x, core), gy: 4 (over z), gz: 2 (over y).
Axes of the slice: x: 2, y: 2, z: 4, core: 2. Of those that a mesh axis runs over, the one named last changes fastest.
Arguments:
- velocity: float32 [3, 32, 128, 512], P(None, 'gz', 'gy', 'gx'), may hold values from -14 to 14, as said below
- geometry: bfloat16 [6, 32, 128, 512], P(None, 'gz', 'gy', 'gx'), may hold values from -0.015 to 0.041, as said below
- mass_weights: bfloat16 [32, 128, 512], P('gz', 'gy', 'gx'), may hold values from 0.0099487305 to 0.099609375
Outputs:
- residual: float32 [3, 32, 128, 512], P(None, 'gz', 'gy', 'gx')
- kinetic: float32 [], replicated
- enstrophy: float32 [], replicated
Inputs may be any that keep to these rules, and one draw needn't show every extreme that they name: `velocity`: coincident points of neighbouring elements hold equal values, and points on the outer boundary of the grid hold zero. `geometry`: at every point the matrix [[g0, g3, g4], [g3, g1, g5], [g4, g5, g2]] is positive definite.
All inputs are finite; a program needn't handle non-finite values.
Results may differ from a plain program's by a relative error of at most 0.0003.
Values sent between devices are 32-bit elements; how exact they have to be, the bound alone decides.
A program may use at most 128 MiB of HBM per device.

v0:
```python
import functools
import itertools

import jax
import jax.numpy as jnp
import numpy as np
from jax import lax
from jax.experimental import pallas as pl
from jax.experimental.pallas import tpu as pltpu
from jax.sharding import PartitionSpec as P

ORDER = 7
PTS = ORDER + 1
MESH = pl.DeviceIdType.MESH
AXES = ("gx", "gy", "gz")
XOFF = [o for o in itertools.product((-1, 0, 1), repeat=3) if o[0] != 0]
YZOFF = [o for o in itertools.product((-1, 0, 1), repeat=3) if o[0] == 0 and o[1] != 0 and o[2] != 0]
YOFF = [(0, -1, 0), (0, 1, 0)]
FACES = YOFF + [(0, 0, -1), (0, 0, 1)]
OFFS = sorted(XOFF + YZOFF, key=lambda o: -sum(map(abs, o)))


def gll_derivative(poly_order):
    node_count = poly_order + 1
    abscissa = np.cos(np.pi * np.arange(node_count) / poly_order)
    legendre = np.zeros((node_count, node_count))
    for newton_step in range(60):
        legendre[:, 0] = 1.0
        legendre[:, 1] = abscissa
        for degree in range(2, node_count):
            legendre[:, degree] = (
                (2 * degree - 1) * abscissa * legendre[:, degree - 1]
                - (degree - 1) * legendre[:, degree - 2]
            ) / degree
        abscissa = abscissa - (abscissa * legendre[:, poly_order] - legendre[:, poly_order - 1]) / (
            node_count * legendre[:, poly_order]
        )
    abscissa = abscissa[::-1]
    end_values = legendre[::-1, poly_order]
    spacing = abscissa[:, None] - abscissa[None, :] + np.eye(node_count)
    deriv_table = end_values[:, None] / end_values[None, :] / spacing
    deriv_table = deriv_table * (1.0 - np.eye(node_count))
    deriv_table[0, 0] = -poly_order * node_count / 4.0
    deriv_table[poly_order, poly_order] = poly_order * node_count / 4.0
    return deriv_table.astype(np.float32)


def split_np(m):
    hi = m.astype(jnp.bfloat16)
    lo = (m - hi.astype(np.float32)).astype(jnp.bfloat16)
    return hi, lo


def tables(rows, cols):
    d = gll_derivative(ORDER)
    out = []
    for mat in (d, d.T):
        hi, lo = split_np(np.kron(np.eye(cols // PTS, dtype=np.float32), mat.T))
        zero = np.zeros_like(lo)
        out.append(np.block([[hi, lo], [hi, zero]]))
        hi, lo = split_np(np.kron(np.eye(PTS * rows // PTS, dtype=np.float32), mat))
        out.append(np.stack([hi, lo]))
    pick = np.zeros((2 * PTS, 2 * cols), np.float32)
    pick[0, [0, cols]] = 1.0
    pick[1, [cols - 1, 2 * cols - 1]] = 1.0
    out.append(pick.astype(jnp.bfloat16))
    put = np.zeros((16, 4 * cols), np.float32)
    for c in range(4):
        for base in (0, 8):
            put[base + c, c * cols + cols - 1] = 1.0
            put[base + 4 + c, c * cols] = 1.0
    out.append(put.astype(jnp.bfloat16))
    return [jnp.asarray(t) for t in out]


def split(x):
    hi = x.astype(jnp.bfloat16)
    lo = (x - hi.astype(jnp.float32)).astype(jnp.bfloat16)
    return hi, lo


def dot(a, b):
    return jnp.dot(a, b, preferred_element_type=jnp.float32)


def along_x(pair, table):
    cols = table.shape[1] // 2
    r = dot(jnp.concatenate(pair, axis=1), table)
    return r[:, :cols] + r[:, cols:]


def along_y(pair, hi, lo):
    cols = pair[0].shape[1]
    r = dot(hi, jnp.concatenate(pair, axis=1))
    return r[:, :cols] + r[:, cols:] + dot(lo, pair[0])


def along_z(planes, mat):
    n = PTS // 2
    mat = mat.astype(np.float64)
    odd = [planes[j] - planes[ORDER - j] for j in range(n)]
    even = [planes[j] + planes[ORDER - j] for j in range(n)]
    low, high = [], []
    for i in range(n):
        p = q = None
        for j in range(n):
            t = odd[j] * float(0.5 * (mat[i, j] - mat[i, ORDER - j]))
            u = even[j] * float(0.5 * (mat[i, j] + mat[i, ORDER - j]))
            p = t if p is None else p + t
            q = u if q is None else q + u
        low.append(p + q)
        high.append(p - q)
    return low + high[::-1]


def kernel(
    sizes,
    v_hbm, g_hbm, m_hbm, dx_hbm, dy_hbm, tx_hbm, ty_hbm, pick_hbm, put_hbm,
    a_out, b_out, s_out,
    v, g, m, dx_ref, dy_ref, tx_ref, ty_ref, pick_ref, put_ref, flux, field, pack, yface, yzrow, rpack, ryface, rzface, ryz, part, parts, zface, keep, halo,
    in_sem, send_sem, recv_sem, ssend, srecv, fsend, frecv,
):
    nx, ny, nz = sizes
    count = nx * ny * nz
    planes, rows, cols = v.shape[1:]
    layers = planes // PTS
    yel = rows // PTS
    half = cols // 2
    ix, iy, iz = (lax.axis_index(a) for a in AXES)
    me = (ix * ny + iy) * nz + iz
    d = gll_derivative(ORDER)

    loads = [
        pltpu.make_async_copy(src, dst, in_sem.at[k])
        for k, (src, dst) in enumerate(
            (
                (m_hbm, m), (pick_hbm, pick_ref), (v_hbm, v), (g_hbm, g), (dx_hbm, dx_ref),
                (dy_hbm, dy_ref), (tx_hbm, tx_ref), (ty_hbm, ty_ref), (put_hbm, put_ref),
            )
        )
    ]
    for c in loads:
        c.start()

    def peer_id(step):
        p = lax.rem(me + step, count)
        return {"gx": p // (ny * nz), "gy": lax.rem(p // nz, ny), "gz": lax.rem(p, nz)}

    def ring(i, n):
        out = [i]
        for _ in range(n - 1):
            t = out[-1] + 1
            out.append(jnp.where(t == n, 0, t))
        return out

    def for_peers(act):
        if count > 64:
            pl.loop(1, count)(lambda step: act(peer_id(step)))
            return
        xs, ys, zs = (ring(i, n) for i, n in zip((ix, iy, iz), sizes))
        for x, y, z in itertools.product(range(nx), range(ny), range(nz)):
            if x or y or z:
                act({"gx": xs[x], "gy": ys[y], "gz": zs[z]})

    barrier = pltpu.get_barrier_semaphore()
    for_peers(
        lambda to: pl.semaphore_signal(barrier, inc=1, device_id=to, device_id_type=MESH)
    )

    n_rows = PTS * rows
    four = (PTS, yel, PTS, cols)
    flat8 = (1, 1, PTS, cols)
    lane = lax.broadcasted_iota(jnp.int32, flat8, 3)
    k_at = lax.broadcasted_iota(jnp.int32, flat8, 2)

    def unit(mask):
        return jnp.where(mask, 1.0, 0.0).astype(jnp.float32)

    x_next = unit((lane % PTS == ORDER) & (lane < cols - 1))
    x_prev = unit((lane % PTS == 0) & (lane > 0))
    y_last = unit(k_at == ORDER)
    y_first = unit(k_at == 0)

    def assemble_xy(x):
        up = pltpu.roll(x, cols - 1, 1).reshape(four)
        down = pltpu.roll(x, 1, 1).reshape(four)
        x = x.reshape(four) + up * x_next + down * x_prev
        flat = x.reshape(PTS * yel, PTS, cols)
        up = pltpu.roll(flat, PTS - 1, 1).reshape(four)
        down = pltpu.roll(flat, 1, 1).reshape(four)
        out = []
        for y in range(yel):
            t = x[:, y:y + 1]
            if y < yel - 1:
                t = t + up[:, y + 1:y + 2] * y_last
            if y > 0:
                t = t + down[:, y - 1:y] * y_first
            out.append(t)
        return jnp.concatenate(out, axis=1).reshape(PTS, rows, cols)

    def finish_channel(c):
        for e in range(1, layers):
            low = field[c, e * PTS - 1]
            high = field[c, e * PTS]
            both = low + high
            field[c, e * PTS - 1] = both
            field[c, e * PTS] = both
        for e in range(layers):
            x = field[c, pl.ds(e * PTS, PTS)].reshape(n_rows, cols)
            r = lax.dot_general(
                pick_ref[...], jnp.concatenate(split(x), axis=1), (((1,), (1,)), ((), ())),
                preferred_element_type=jnp.float32,
            )
            for s in range(2):
                pack[s, pl.ds(c, 1), pl.ds(e * n_rows, n_rows)] = r[s:s + 1]
        for side, y in ((0, 0), (1, rows - 1)):
            face = field[c, :, y, :]
            yface[side, c] = face
            yzrow[side, 0, c] = face[0:1]
            yzrow[side, 1, c] = face[planes - 1:planes]
        zface[0, c] = field[c, 0]
        zface[1, c] = field[c, planes - 1]

    total_rows = planes * rows
    here = (ix, iy, iz)

    def there(off):
        ok = None
        for o, i, n in zip(off, here, sizes):
            if o:
                t = (i > 0) if o < 0 else (i < n - 1)
                ok = t if ok is None else ok & t
        return ok

    def side(o):
        return (o + 1) // 2

    def target(off):
        return {a: i + o for a, i, o in zip(AXES, here, off)}

    def part_of(dz):
        width = total_rows // layers // 2
        width = width if width % 128 == 0 else total_rows
        if dz == 0:
            return pl.ds(0, total_rows)
        return pl.ds(0 if dz < 0 else total_rows - width, width)

    def landing(off):
        if off[0]:
            return rpack.at[XOFF.index(off), :, part_of(-off[2])]
        return ryz.at[YZOFF.index(off)]

    def copy_to(off):
        opp = tuple(-o for o in off)
        if off[0]:
            src = pack.at[side(off[0]), :, part_of(off[2])]
        else:
            src = yzrow.at[side(off[1]), side(off[2])]
        return pltpu.make_async_remote_copy(
            src_ref=src, dst_ref=landing(opp), send_sem=send_sem.at[OFFS.index(off)],
            recv_sem=recv_sem.at[OFFS.index(opp)], device_id=target(off), device_id_type=MESH,
        )

    def face_copy(off, c):
        k, opp = FACES.index(off), FACES.index(tuple(-o for o in off))
        src, dst = (yface, ryface) if off[1] else (zface, rzface)
        return pltpu.make_async_remote_copy(
            src_ref=src.at[k % 2, c], dst_ref=dst.at[opp % 2, c], send_sem=fsend.at[k, c],
            recv_sem=frecv.at[opp, c], device_id=target(off), device_id_type=MESH,
        )

    def send_faces(c):
        for off in FACES[::-1]:
            @pl.when(there(off))
            def _(off=off):
                face_copy(off, c).start()

    inner_x = unit(((lane > 0) | (ix > 0)) & ((lane < cols - 1) | (ix < nx - 1))).reshape(1, PTS, cols)
    z3 = lax.broadcasted_iota(jnp.int32, (planes, 1, cols), 0)
    inner_z = unit(((z3 > 0) | (iz > 0)) & ((z3 < planes - 1) | (iz < nz - 1)))
    for y in range(yel):
        w = inner_x
        if y == 0:
            w = w * unit((k_at > 0) | (iy > 0)).reshape(1, PTS, cols)
        if y == yel - 1:
            w = w * unit((k_at < ORDER) | (iy < ny - 1)).reshape(1, PTS, cols)
        keep[:, y * PTS:(y + 1) * PTS, :] = w * inner_z
    loads[0].wait()
    loads[1].wait()
    for e in range(layers):
        x = m[pl.ds(e * PTS, PTS)].astype(jnp.float32).reshape(PTS * rows, cols)
        field[3, pl.ds(e * PTS, PTS)] = assemble_xy(x)
    finish_channel(3)
    for c in loads[2:]:
        c.wait()

    def gradients(e, acc):
        kin, ens = acc
        at = pl.ds(pl.multiple_of(e * PTS, PTS), PTS)
        mass = m[at].astype(jnp.float32)
        g0, g1, g2, g3, g4, g5 = (g[k, at].astype(jnp.float32) for k in range(6))
        for c in range(3):
            block = v[c, at]
            flat = block.reshape(PTS * rows, cols)
            kin = kin + jnp.sum((mass * block * block).reshape(-1, PTS, cols), axis=0)
            pair = split(flat)
            gr = along_x(pair, dx_ref[...]).reshape(block.shape)
            gs = along_y(pair, dy_ref[0], dy_ref[1]).reshape(block.shape)
            gt = jnp.stack(along_z([block[z] for z in range(PTS)], d))
            fr = g0 * gr + g3 * gs + g4 * gt
            fs = g3 * gr + g1 * gs + g5 * gt
            ft = g4 * gr + g5 * gs + g2 * gt
            ens = ens + jnp.sum((gr * fr + gs * fs + gt * ft).reshape(-1, PTS, cols), axis=0)
            flux[0, c, at] = fr
            flux[1, c, at] = fs
            flux[2, c, at] = ft
        return kin, ens

    zero = jnp.zeros((PTS, cols), jnp.float32)
    kin, ens = lax.fori_loop(0, layers, gradients, (zero, zero))
    mine = jnp.concatenate(
        [jnp.sum(kin, 0, keepdims=True) * 0.5, jnp.sum(ens, 0, keepdims=True)], axis=0
    )
    part[...] = mine
    parts[me] = mine

    pl.semaphore_wait(barrier, count - 1)

    def scalar_copy(to):
        return pltpu.make_async_remote_copy(
            src_ref=part, dst_ref=parts.at[me], send_sem=ssend, recv_sem=srecv,
            device_id=to, device_id_type=MESH,
        )

    for_peers(lambda to: scalar_copy(to).start())
    send_faces(3)

    @pl.loop(0, 3)
    def _(c):
        for e in range(layers):
            at = pl.ds(e * PTS, PTS)
            fr = flux[0, c, at].reshape(PTS * rows, cols)
            fs = flux[1, c, at].reshape(PTS * rows, cols)
            ft = flux[2, c, at]
            x = along_x(split(fr), tx_ref[...]) + along_y(split(fs), ty_ref[0], ty_ref[1])
            z = jnp.stack(along_z([ft[k] for k in range(PTS)], d.T))
            field[c, at] = assemble_xy(x + z.reshape(x.shape))
        finish_channel(c)
        send_faces(c)

    for off in OFFS:
        @pl.when(there(off))
        def _(off=off):
            copy_to(off).start()

    for off in OFFS:
        @pl.when(there(off))
        def _(off=off):
            dst = landing(off)
            pltpu.make_async_copy(dst, dst, recv_sem.at[OFFS.index(off)]).wait()

    for k, off in enumerate(FACES):
        @pl.when(there(off))
        def _(k=k, off=off):
            for c in range(4):
                dst = (ryface if off[1] else rzface).at[k % 2, c]
                pltpu.make_async_copy(dst, dst, frecv.at[k, c]).wait()

    pshape = (4, total_rows)
    place = lax.broadcasted_iota(jnp.int32, (1, total_rows), 1)
    for s, dx in ((0, 1), (1, -1)):
        acc = jnp.zeros(pshape, jnp.float32)
        for off in XOFF:
            if off[0] != dx:
                continue
            x = rpack[XOFF.index(off)]
            hit = place >= 0
            shift = 0
            if off[1]:
                hit = hit & (place % rows == (0 if off[1] < 0 else rows - 1))
                shift += off[1] * (rows - 1)
            if off[2]:
                hit = hit & (place // rows == (0 if off[2] < 0 else planes - 1))
                shift += off[2] * (planes - 1) * rows
            if shift:
                x = pltpu.roll(x, shift % total_rows, 1)
            acc = acc + jnp.where(jnp.broadcast_to(hit & there(off), pshape), x, 0.0)
        hi, lo = split(acc)
        halo[s * 4:s * 4 + 4, :] = hi.astype(jnp.float32)
        halo[8 + s * 4:12 + s * 4, :] = lo.astype(jnp.float32)

    z1 = lax.broadcasted_iota(jnp.int32, (planes, cols), 0)

    def add_yz(c):
        for dy, y in ((-1, 0), (1, rows - 1)):
            acc = jnp.where(there((0, dy, 0)), ryface[YOFF.index((0, dy, 0)), c], 0.0)
            for dz, z in ((-1, 0), (1, planes - 1)):
                off = (0, dy, dz)
                acc = acc + jnp.where((z1 == z) & there(off), ryz[YZOFF.index(off), c], 0.0)
            field[c, :, y, :] = field[c, :, y, :] + acc
        for k, (dz, z) in enumerate(((-1, 0), (1, planes - 1))):
            field[c, z] = field[c, z] + jnp.where(there((0, 0, dz)), rzface[k, c], 0.0)

    for c in range(4):
        add_yz(c)
    halos = halo[...].astype(jnp.bfloat16)
    for e in range(layers):
        at = pl.ds(e * PTS, PTS)
        x = lax.dot_general(
            halos[:, e * n_rows:(e + 1) * n_rows], put_ref[...], (((0,), (0,)), ((), ())),
            preferred_element_type=jnp.float32,
        )
        w = keep[at]
        mass = (field[3, at] + x[:, 3 * cols:].reshape(PTS, rows, cols)) * w
        for c in range(3):
            a_out[c, at] = (field[c, at] + x[:, c * cols:(c + 1) * cols].reshape(PTS, rows, cols)) * w
            b_out[c, at] = mass * v[c, at]

    rest = parts.at[pl.ds(0, count - 1)]
    pltpu.make_async_copy(rest, rest, srecv).wait()
    total = jnp.sum(parts[...], axis=0)
    total = jnp.sum(total, axis=1, keepdims=True)
    s_out[...] = jnp.broadcast_to(total, (2, cols))

    for off in OFFS:
        @pl.when(there(off))
        def _(off=off):
            copy_to(off).wait_send()

    for off in FACES:
        @pl.when(there(off))
        def _(off=off):
            for c in range(4):
                face_copy(off, c).wait_send()

    sent = parts.at[pl.ds(0, count - 1)]
    pltpu.make_async_copy(sent, sent, ssend).wait()


def finish(a_ref, b_ref, s_ref, r_hbm, k_hbm, e_hbm, r, k, e, sem):
    chunks = r.shape[0]
    kin = s_ref[0:1, 0:1]
    ens = s_ref[1:2, 0:1]
    rayleigh = ens / (2.0 * kin)
    k[...] = kin
    e[...] = ens
    outs = [
        pltpu.make_async_copy(k, k_hbm, sem.at[chunks]),
        pltpu.make_async_copy(e, e_hbm, sem.at[chunks + 1]),
    ]
    for c in range(chunks):
        r[c] = a_ref[c] - rayleigh[None] * b_ref[c]
        outs.append(pltpu.make_async_copy(r.at[c], r_hbm.at[c], sem.at[c]))
        outs[-1].start()
    outs[0].start()
    outs[1].start()
    for c in outs:
        c.wait()


def per_device(sizes, velocity, geometry, mass_weights):
    planes, rows, cols = mass_weights.shape
    f32 = jnp.float32
    count = sizes[0] * sizes[1] * sizes[2]
    vmem = pl.BlockSpec(memory_space=pltpu.VMEM)
    hbm = pl.BlockSpec(memory_space=pltpu.HBM)
    consts = tables(rows, cols)
    applied, weighted, scalars = pl.pallas_call(
        functools.partial(kernel, sizes),
        out_shape=(
            jax.ShapeDtypeStruct(velocity.shape, f32),
            jax.ShapeDtypeStruct(velocity.shape, f32),
            jax.ShapeDtypeStruct((2, cols), f32),
        ),
        in_specs=[hbm] * 9,
        out_specs=(vmem, vmem, vmem),
        scratch_shapes=[
            pltpu.VMEM(velocity.shape, f32),
            pltpu.VMEM(geometry.shape, geometry.dtype),
            pltpu.VMEM(mass_weights.shape, mass_weights.dtype),
            *[pltpu.VMEM(t.shape, t.dtype) for t in consts],
            pltpu.VMEM((3,) + velocity.shape, f32),
            pltpu.VMEM((4, planes, rows, cols), f32),
            pltpu.VMEM((2, 4, planes * rows), f32),
            pltpu.VMEM((2, 4, planes, cols), f32),
            pltpu.VMEM((2, 2, 4, 1, cols), f32),
            pltpu.VMEM((len(XOFF), 4, planes * rows), f32),
            pltpu.VMEM((2, 4, planes, cols), f32),
            pltpu.VMEM((2, 4, rows, cols), f32),
            pltpu.VMEM((len(YZOFF), 4, 1, cols), f32),
            pltpu.VMEM((2, cols), f32),
            pltpu.VMEM((count, 2, cols), f32),
            pltpu.VMEM((2, 4, rows, cols), f32),
            pltpu.VMEM(mass_weights.shape, f32),
            pltpu.VMEM((16, planes * rows), f32),
            pltpu.SemaphoreType.DMA((9,)),
            pltpu.SemaphoreType.DMA((len(OFFS),)),
            pltpu.SemaphoreType.DMA((len(OFFS),)),
            pltpu.SemaphoreType.DMA,
            pltpu.SemaphoreType.DMA,
            pltpu.SemaphoreType.DMA((len(FACES), 4)),
            pltpu.SemaphoreType.DMA((len(FACES), 4)),
        ],
        compiler_params=pltpu.CompilerParams(
            collective_id=0, has_side_effects=True, vmem_limit_bytes=32 * 1024 * 1024
        ),
    )(*(pltpu.with_memory_space_constraint(t, pltpu.HBM) for t in (velocity, geometry, mass_weights, *consts)))
    one = jax.ShapeDtypeStruct((1, 1), f32)
    residual, kinetic, enstrophy = pl.pallas_call(
        finish,
        out_shape=(jax.ShapeDtypeStruct(velocity.shape, f32), one, one),
        in_specs=[vmem] * 3,
        out_specs=(hbm,) * 3,
        scratch_shapes=[
            pltpu.VMEM(velocity.shape, f32),
            pltpu.VMEM((1, 1), f32),
            pltpu.VMEM((1, 1), f32),
            pltpu.SemaphoreType.DMA((velocity.shape[0] + 2,)),
        ],
        compiler_params=pltpu.CompilerParams(vmem_limit_bytes=8 * 1024 * 1024),
    )(applied, weighted, scalars)
    return residual, kinetic[0, 0], enstrophy[0, 0]


def solution(mesh):
    sizes = tuple(mesh.shape[a] for a in AXES)
    in_specs = (P(None, "gz", "gy", "gx"), P(None, "gz", "gy", "gx"), P("gz", "gy", "gx"))
    out_specs = (P(None, "gz", "gy", "gx"), P(), P())
    return jax.shard_map(
        functools.partial(per_device, sizes),
        mesh=mesh, in_specs=in_specs, out_specs=out_specs, check_vma=False,
    )
```

profile of v0, /device:TPU:0, one launch (start us, length us, event | category | flops | bytes accessed | tf_op | source)
XLA Modules:
  0.0 14.6 jit_solution(17312265406770165355)
XLA Ops:
  0.6 13.0 %shard_map.112 = (f32[3,16,32,128]{3,2,1,0:T(8,128)S(1)}, f32[3,16,32,128]{3,2,1,0:T(8,128)S(1)}, f32[2,128]{1,0:T(2,128)S(1)}) custom-call(f32[3,16,32,128]{3,2,1,0:T(8,128)} %v_hbm.1, bf16[6,16,32,128]{3,2,1,0:T(8,128)(2,1)} %g_hbm.1, bf16[16,32,128]{2,1,0:T(8,128)(2,1)} %m_hbm.1, bf16[256,256]{1,0:T(8,128)(2,1)} %constant.12.clone.dx_hbm, ...), custom_call_target="tpu_custom_call" | custom-call | tf_op jit(solution)/shard_map/pallas_call | solution.py:468
  13.6 1.0 %shard_map.113 = (f32[3,16,32,128]{3,2,1,0:T(8,128)}, f32[1,1]{1,0:T(1,128)}, f32[1,1]{1,0:T(1,128)}) custom-call(f32[3,16,32,128]{3,2,1,0:T(8,128)S(1)} %get-tuple-element.9.a_ref, f32[3,16,32,128]{3,2,1,0:T(8,128)S(1)} %get-tuple-element.10.b_ref, f32[2,128]{1,0:T(2,128)S(1)} %get-tuple-element.11.s_ref), custom_call_target="tpu_custom_call" | custom-call | tf_op jit(solution)/shard_map/pallas_call | solution.py:509
where the time goes:
time: 14.7 us; the launch traced here: 14.6 us
  Pallas kernels  14 us (95%)
  between operations  0.64 us (4%)
    pallas_call x1, Pallas kernels, per_device(): pl.pallas_call(functools.partial(kernel, sizes), out_shape=(jax.ShapeDtyp...  13 us
    pallas_call x1, Pallas kernels, per_device(): pl.pallas_call(finish, out_shape=(jax.ShapeDtypeStruct(velocity.shape, f3...  1 us

commit v1 on v0

--- a/solution.py
+++ b/solution.py
@@ -51,15 +51,16 @@
     return hi, lo
 
 
-def tables(rows, cols):
+def tables(cols):
     d = gll_derivative(ORDER)
+    eye = np.eye(PTS, dtype=np.float32)
     out = []
     for mat in (d, d.T):
         hi, lo = split_np(np.kron(np.eye(cols // PTS, dtype=np.float32), mat.T))
         zero = np.zeros_like(lo)
         out.append(np.block([[hi, lo], [hi, zero]]))
-        hi, lo = split_np(np.kron(np.eye(PTS * rows // PTS, dtype=np.float32), mat))
-        out.append(np.stack([hi, lo]))
+        hi, lo = split_np(np.concatenate([np.kron(eye, mat), np.kron(mat, eye)]))
+        out.append(np.concatenate([hi, hi, lo, lo], axis=1))
     pick = np.zeros((2 * PTS, 2 * cols), np.float32)
     pick[0, [0, cols]] = 1.0
     pick[1, [cols - 1, 2 * cols - 1]] = 1.0
@@ -89,83 +90,96 @@
     return r[:, :cols] + r[:, cols:]
 
 
-def along_y(pair, hi, lo):
-    cols = pair[0].shape[1]
-    r = dot(hi, jnp.concatenate(pair, axis=1))
-    return r[:, :cols] + r[:, cols:] + dot(lo, pair[0])
-
-
-def along_z(planes, mat):
-    n = PTS // 2
-    mat = mat.astype(np.float64)
-    odd = [planes[j] - planes[ORDER - j] for j in range(n)]
-    even = [planes[j] + planes[ORDER - j] for j in range(n)]
-    low, high = [], []
-    for i in range(n):
-        p = q = None
-        for j in range(n):
-            t = odd[j] * float(0.5 * (mat[i, j] - mat[i, ORDER - j]))
-            u = even[j] * float(0.5 * (mat[i, j] + mat[i, ORDER - j]))
-            p = t if p is None else p + t
-            q = u if q is None else q + u
-        low.append(p + q)
-        high.append(p - q)
-    return low + high[::-1]
+def stacked(pairs):
+    hi = jnp.concatenate([p[0] for p in pairs], axis=1)
+    lo = jnp.concatenate([p[1] for p in pairs], axis=1)
+    return jnp.concatenate([hi, lo, hi, lo], axis=0)
 
 
 def kernel(
     sizes,
-    v_hbm, g_hbm, m_hbm, dx_hbm, dy_hbm, tx_hbm, ty_hbm, pick_hbm, put_hbm,
+    v_hbm, g_hbm, m_hbm, dx_hbm, dyz_hbm, tx_hbm, tyz_hbm, pick_hbm, put_hbm,
     a_out, b_out, s_out,
-    v, g, m, dx_ref, dy_ref, tx_ref, ty_ref, pick_ref, put_ref, flux, field, pack, yface, yzrow, rpack, ryface, rzface, ryz, part, parts, zface, keep, halo,
-    in_sem, send_sem, recv_sem, ssend, srecv, fsend, frecv,
+    v, g, m, dx_ref, dyz_ref, tx_ref, tyz_ref, pick_ref, put_ref, flux, field, pack, yface, yzrow, rpack, ryface, rzface, ryz, part, parts, low, zface, keep, halo,
+    in_sem, send_sem, recv_sem, ssend, srecv, lsend, lrecv, fsend, frecv,
 ):
     nx, ny, nz = sizes
     count = nx * ny * nz
     planes, rows, cols = v.shape[1:]
     layers = planes // PTS
     yel = rows // PTS
-    half = cols // 2
     ix, iy, iz = (lax.axis_index(a) for a in AXES)
-    me = (ix * ny + iy) * nz + iz
-    d = gll_derivative(ORDER)
-
-    loads = [
-        pltpu.make_async_copy(src, dst, in_sem.at[k])
-        for k, (src, dst) in enumerate(
-            (
-                (m_hbm, m), (pick_hbm, pick_ref), (v_hbm, v), (g_hbm, g), (dx_hbm, dx_ref),
-                (dy_hbm, dy_ref), (tx_hbm, tx_ref), (ty_hbm, ty_ref), (put_hbm, put_ref),
-            )
+    half = ny // 2
+    n_low = half * nx * nz
+    is_low = iy < half
+    is_up = iy >= half
+
+    def start(pairs, k):
+        cs = [pltpu.make_async_copy(s, d, in_sem.at[k + i]) for i, (s, d) in enumerate(pairs)]
+        for c in cs:
+            c.start()
+        return cs
+
+    tabs = start([(dx_hbm, dx_ref), (dyz_hbm, dyz_ref)], 0)
+    loads = []
+    for e in range(layers):
+        at = pl.ds(e * PTS, PTS)
+        k = 2 + 3 * e
+        loads.append(
+            start([(v_hbm.at[:, at], v.at[:, at]), (m_hbm.at[at], m.at[at]), (g_hbm.at[:, at], g.at[:, at])], k)
         )
-    ]
-    for c in loads:
-        c.start()
-
-    def peer_id(step):
-        p = lax.rem(me + step, count)
-        return {"gx": p // (ny * nz), "gy": lax.rem(p // nz, ny), "gz": lax.rem(p, nz)}
-
-    def ring(i, n):
-        out = [i]
-        for _ in range(n - 1):
-            t = out[-1] + 1
-            out.append(jnp.where(t == n, 0, t))
-        return out
-
-    def for_peers(act):
+    late_tabs = start(
+        [(tx_hbm, tx_ref), (tyz_hbm, tyz_ref), (pick_hbm, pick_ref), (put_hbm, put_ref)], 2 + 3 * layers
+    )
+
+    def rank(x, y, z):
+        return (y * nx + x) * nz + z
+
+    me = rank(ix, iy, iz)
+
+    def for_targets(ys, act):
         if count > 64:
-            pl.loop(1, count)(lambda step: act(peer_id(step)))
+            def body(t):
+                y, x, z = t // (nx * nz), lax.rem(t // nz, nx), lax.rem(t, nz)
+                act((x, y, z), t != me)
+            pl.loop(ys[0] * nx * nz, (ys[-1] + 1) * nx * nz)(body)
             return
-        xs, ys, zs = (ring(i, n) for i, n in zip((ix, iy, iz), sizes))
-        for x, y, z in itertools.product(range(nx), range(ny), range(nz)):
-            if x or y or z:
-                act({"gx": xs[x], "gy": ys[y], "gz": zs[z]})
+        for y, x, z in itertools.product(ys, range(nx), range(nz)):
+            act((x, y, z), rank(x, y, z) != me)
+
+    lows, ups = range(half), range(half, ny)
+
+    def dev(t):
+        return dict(zip(AXES, t))
 
     barrier = pltpu.get_barrier_semaphore()
-    for_peers(
-        lambda to: pl.semaphore_signal(barrier, inc=1, device_id=to, device_id_type=MESH)
-    )
+
+    def greet(t):
+        pl.semaphore_signal(barrier, inc=1, device_id=dev(t), device_id_type=MESH)
+
+    def greet_if(t, ok):
+        pl.when(ok)(lambda: greet(t))
+
+    def greet_low(t, ok):
+        x, y, z = t
+        near = (jnp.abs(ix - x) <= 1) & (jnp.abs(iz - z) <= 1) & (iy - y == 1)
+        pl.when(near)(lambda: greet(t))
+
+    for_targets(ups, greet_if)
+
+    @pl.when(is_low)
+    def _():
+        for_targets(lows, greet_if)
+
+    @pl.when(is_up)
+    def _():
+        for_targets(lows, greet_low)
+
+    def cross(i, n):
+        return 1 + jnp.where(i > 0, 1, 0) + jnp.where(i < n - 1, 1, 0)
+
+    beyond = jnp.where(iy == half - 1, cross(ix, nx) * cross(iz, nz), 0)
+    heard = jnp.where(is_low, n_low - 1 + beyond, count - 1)
 
     n_rows = PTS * rows
     four = (PTS, yel, PTS, cols)
@@ -181,22 +195,28 @@
     y_last = unit(k_at == ORDER)
     y_first = unit(k_at == 0)
 
-    def assemble_xy(x):
-        up = pltpu.roll(x, cols - 1, 1).reshape(four)
-        down = pltpu.roll(x, 1, 1).reshape(four)
-        x = x.reshape(four) + up * x_next + down * x_prev
-        flat = x.reshape(PTS * yel, PTS, cols)
-        up = pltpu.roll(flat, PTS - 1, 1).reshape(four)
-        down = pltpu.roll(flat, 1, 1).reshape(four)
+    def assemble_xy(blocks):
+        tiles = (PTS, PTS, cols)
+        lane_next, lane_prev = x_next.reshape(1, PTS, cols), x_prev.reshape(1, PTS, cols)
+        last, first = y_last.reshape(1, PTS, cols), y_first.reshape(1, PTS, cols)
+        xs = []
+        for x in blocks:
+            up = pltpu.roll(x, cols - 1, 1).reshape(tiles)
+            down = pltpu.roll(x, 1, 1).reshape(tiles)
+            xs.append(x.reshape(tiles) + up * lane_next + down * lane_prev)
         out = []
         for y in range(yel):
-            t = x[:, y:y + 1]
+            t = xs[y]
             if y < yel - 1:
-                t = t + up[:, y + 1:y + 2] * y_last
+                t = t + pltpu.roll(xs[y + 1], PTS - 1, 1) * last
             if y > 0:
-                t = t + down[:, y - 1:y] * y_first
+                t = t + pltpu.roll(xs[y - 1], 1, 1) * first
             out.append(t)
-        return jnp.concatenate(out, axis=1).reshape(PTS, rows, cols)
+        return out
+
+    def put_field(c, e, blocks):
+        for y, t in enumerate(assemble_xy(blocks)):
+            field[c, pl.ds(e * PTS, PTS), y * PTS:(y + 1) * PTS, :] = t
 
     def finish_channel(c):
         for e in range(1, layers):
@@ -285,73 +305,135 @@
         if y == yel - 1:
             w = w * unit((k_at < ORDER) | (iy < ny - 1)).reshape(1, PTS, cols)
         keep[:, y * PTS:(y + 1) * PTS, :] = w * inner_z
-    loads[0].wait()
-    loads[1].wait()
+    for c in tabs:
+        c.wait()
+    zero = jnp.zeros((PTS, cols), jnp.float32)
+    kin, ens = zero, zero
+    n_blk = PTS * PTS
     for e in range(layers):
-        x = m[pl.ds(e * PTS, PTS)].astype(jnp.float32).reshape(PTS * rows, cols)
-        field[3, pl.ds(e * PTS, PTS)] = assemble_xy(x)
-    finish_channel(3)
-    for c in loads[2:]:
-        c.wait()
-
-    def gradients(e, acc):
-        kin, ens = acc
-        at = pl.ds(pl.multiple_of(e * PTS, PTS), PTS)
+        for c in loads[e]:
+            c.wait()
+        at = pl.ds(e * PTS, PTS)
         mass = m[at].astype(jnp.float32)
-        g0, g1, g2, g3, g4, g5 = (g[k, at].astype(jnp.float32) for k in range(6))
+        geo = [g[k, at].astype(jnp.float32) for k in range(6)]
+        square = None
         for c in range(3):
             block = v[c, at]
-            flat = block.reshape(PTS * rows, cols)
-            kin = kin + jnp.sum((mass * block * block).reshape(-1, PTS, cols), axis=0)
-            pair = split(flat)
-            gr = along_x(pair, dx_ref[...]).reshape(block.shape)
-            gs = along_y(pair, dy_ref[0], dy_ref[1]).reshape(block.shape)
-            gt = jnp.stack(along_z([block[z] for z in range(PTS)], d))
-            fr = g0 * gr + g3 * gs + g4 * gt
-            fs = g3 * gr + g1 * gs + g5 * gt
-            ft = g4 * gr + g5 * gs + g2 * gt
-            ens = ens + jnp.sum((gr * fr + gs * fs + gt * ft).reshape(-1, PTS, cols), axis=0)
-            flux[0, c, at] = fr
-            flux[1, c, at] = fs
-            flux[2, c, at] = ft
-        return kin, ens
-
-    zero = jnp.zeros((PTS, cols), jnp.float32)
-    kin, ens = lax.fori_loop(0, layers, gradients, (zero, zero))
+            sq = block * block
+            square = sq if square is None else square + sq
+            blks = [block[:, y * PTS:(y + 1) * PTS, :].reshape(n_blk, cols) for y in range(yel)]
+            pairs = [split(b) for b in blks]
+            whole = tuple(jnp.concatenate([p[s] for p in pairs], axis=0) for s in range(2))
+            gr_all = along_x(whole, dx_ref[...])
+            for y0 in range(0, yel, 2):
+                r = dot(dyz_ref[...], stacked(pairs[y0:y0 + 2]))
+                for s in range(2):
+                    y = y0 + s
+                    tile = (PTS, PTS, cols)
+                    gr = gr_all[y * n_blk:(y + 1) * n_blk].reshape(tile)
+                    gs = r[:n_blk, s * cols:(s + 1) * cols].reshape(tile)
+                    gt = r[n_blk:, s * cols:(s + 1) * cols].reshape(tile)
+                    g0, g1, g2, g3, g4, g5 = (t[:, y * PTS:(y + 1) * PTS, :] for t in geo)
+                    fr = g0 * gr + g3 * gs + g4 * gt
+                    fs = g3 * gr + g1 * gs + g5 * gt
+                    ft = g4 * gr + g5 * gs + g2 * gt
+                    ens = ens + jnp.sum(gr * fr + gs * fs + gt * ft, axis=0)
+                    flux[0, c, e, y] = fr
+                    flux[1, c, e, y] = fs
+                    flux[2, c, e, y] = ft
+        kin = kin + jnp.sum((mass * square).reshape(-1, PTS, cols), axis=0)
     mine = jnp.concatenate(
         [jnp.sum(kin, 0, keepdims=True) * 0.5, jnp.sum(ens, 0, keepdims=True)], axis=0
     )
     part[...] = mine
-    parts[me] = mine
-
-    pl.semaphore_wait(barrier, count - 1)
+
+    kind = jnp.where(is_up, 1, 0)
 
     def scalar_copy(to):
         return pltpu.make_async_remote_copy(
-            src_ref=part, dst_ref=parts.at[me], send_sem=ssend, recv_sem=srecv,
+            src_ref=part, dst_ref=parts.at[me], send_sem=ssend, recv_sem=srecv.at[kind],
             device_id=to, device_id_type=MESH,
         )
 
-    for_peers(lambda to: scalar_copy(to).start())
-    send_faces(3)
+    def tell(t, ok):
+        pl.when(ok)(lambda: scalar_copy(dev(t)).start())
+
+    def meet():
+        pl.semaphore_wait(barrier, heard)
+        for_targets(lows, tell)
+
+        @pl.when(is_up)
+        def _():
+            for_targets(ups, tell)
+
+    across = (nx - 1) // 2 - ix // 2 + (nz - 1 - iz)
+    ahead = across + jnp.where(is_low, half - 1 - iy, ny - 1 - iy)
+    turn = jnp.where((ix % 2 == 1) & (ix < nx - 1), 1, 0) + jnp.where(iz < nz - 1, 1, 0)
+    ahead = jnp.where(iy == half - 1, jnp.maximum(ahead, 1 + turn), ahead)
+    slot = jnp.where(ahead <= 1, -1, jnp.where(ahead == 2, 0, 2))
+
+    @pl.when(slot < 0)
+    def _():
+        meet()
+    parts[me] = mine
+
+    for c in late_tabs:
+        c.wait()
+    for e in range(layers):
+        x = m[pl.ds(e * PTS, PTS)].astype(jnp.float32)
+        put_field(3, e, [x[:, y * PTS:(y + 1) * PTS, :].reshape(n_blk, cols) for y in range(yel)])
+    finish_channel(3)
 
     @pl.loop(0, 3)
     def _(c):
         for e in range(layers):
-            at = pl.ds(e * PTS, PTS)
-            fr = flux[0, c, at].reshape(PTS * rows, cols)
-            fs = flux[1, c, at].reshape(PTS * rows, cols)
-            ft = flux[2, c, at]
-            x = along_x(split(fr), tx_ref[...]) + along_y(split(fs), ty_ref[0], ty_ref[1])
-            z = jnp.stack(along_z([ft[k] for k in range(PTS)], d.T))
-            field[c, at] = assemble_xy(x + z.reshape(x.shape))
+            fr, fs, ft = ([split(flux[k, c, e, y].reshape(n_blk, cols)) for y in range(yel)] for k in range(3))
+            whole = tuple(jnp.concatenate([p[s] for p in fr], axis=0) for s in range(2))
+            x = along_x(whole, tx_ref[...])
+            blocks = []
+            for y0 in range(0, yel, 2):
+                r = dot(tyz_ref[0:n_blk], stacked(fs[y0:y0 + 2])) + dot(tyz_ref[n_blk:], stacked(ft[y0:y0 + 2]))
+                for s in range(2):
+                    y = y0 + s
+                    blocks.append(x[y * n_blk:(y + 1) * n_blk] + r[:, s * cols:(s + 1) * cols])
+            put_field(c, e, blocks)
         finish_channel(c)
-        send_faces(c)
+        pl.when(slot == c)(meet)
 
     for off in OFFS:
         @pl.when(there(off))
         def _(off=off):
             copy_to(off).start()
+
+    for c in range(4):
+        send_faces(c)
+
+    def relay():
+        return pltpu.make_async_remote_copy(
+            src_ref=low, dst_ref=low, send_sem=lsend, recv_sem=lrecv,
+            device_id={"gx": ix, "gy": iy + 1, "gz": iz}, device_id_type=MESH,
+        )
+
+    def wait_rows(n, sem):
+        rest = parts.at[pl.ds(0, n)]
+        pltpu.make_async_copy(rest, rest, sem).wait()
+
+    def low_sum():
+        wait_rows(n_low - 1, srecv.at[0])
+        low[...] = jnp.sum(parts[0:n_low], axis=0)
+
+    def low_wait():
+        pltpu.make_async_copy(low, low, lrecv).wait()
+
+    @pl.when(iy == half - 1)
+    def _():
+        low_sum()
+        relay().start()
+
+    @pl.when(is_up & (iy < ny - 1))
+    def _():
+        low_wait()
+        relay().start()
 
     for off in OFFS:
         @pl.when(there(off))
@@ -416,12 +498,6 @@
             a_out[c, at] = (field[c, at] + x[:, c * cols:(c + 1) * cols].reshape(PTS, rows, cols)) * w
             b_out[c, at] = mass * v[c, at]
 
-    rest = parts.at[pl.ds(0, count - 1)]
-    pltpu.make_async_copy(rest, rest, srecv).wait()
-    total = jnp.sum(parts[...], axis=0)
-    total = jnp.sum(total, axis=1, keepdims=True)
-    s_out[...] = jnp.broadcast_to(total, (2, cols))
-
     for off in OFFS:
         @pl.when(there(off))
         def _(off=off):
@@ -433,17 +509,48 @@
             for c in range(4):
                 face_copy(off, c).wait_send()
 
-    sent = parts.at[pl.ds(0, count - 1)]
-    pltpu.make_async_copy(sent, sent, ssend).wait()
+    n_up = count - n_low
+
+    @pl.when(is_low)
+    def _():
+        wait_rows(n_low - 1, ssend)
+
+    @pl.when(is_low & (iy < half - 1))
+    def _():
+        low_sum()
+
+    @pl.when(is_up)
+    def _():
+        wait_rows(count - 1, ssend)
+
+    @pl.when(iy == ny - 1)
+    def _():
+        low_wait()
+
+    @pl.when((iy >= half - 1) & (iy < ny - 1))
+    def _():
+        relay().wait_send()
+
+    @pl.when(is_low)
+    def _():
+        wait_rows(n_up, srecv.at[1])
+
+    @pl.when(is_up)
+    def _():
+        wait_rows(n_up - 1, srecv.at[1])
+
+    total = jnp.sum(parts[n_low:count], axis=0) + low[...]
+    total = jnp.sum(total, axis=1, keepdims=True)
+    s_out[...] = jnp.broadcast_to(total, (2, cols))
 
 
 def finish(a_ref, b_ref, s_ref, r_hbm, k_hbm, e_hbm, r, k, e, sem):
     chunks = r.shape[0]
-    kin = s_ref[0:1, 0:1]
-    ens = s_ref[1:2, 0:1]
+    kin = s_ref[0:1, :]
+    ens = s_ref[1:2, :]
     rayleigh = ens / (2.0 * kin)
-    k[...] = kin
-    e[...] = ens
+    k[...] = kin[:, 0:1]
+    e[...] = ens[:, 0:1]
     outs = [
         pltpu.make_async_copy(k, k_hbm, sem.at[chunks]),
         pltpu.make_async_copy(e, e_hbm, sem.at[chunks + 1]),
@@ -464,7 +571,8 @@
     count = sizes[0] * sizes[1] * sizes[2]
     vmem = pl.BlockSpec(memory_space=pltpu.VMEM)
     hbm = pl.BlockSpec(memory_space=pltpu.HBM)
-    consts = tables(rows, cols)
+    consts = tables(cols)
+    layers = planes // PTS
     applied, weighted, scalars = pl.pallas_call(
         functools.partial(kernel, sizes),
         out_shape=(
@@ -479,7 +587,7 @@
             pltpu.VMEM(geometry.shape, geometry.dtype),
             pltpu.VMEM(mass_weights.shape, mass_weights.dtype),
             *[pltpu.VMEM(t.shape, t.dtype) for t in consts],
-            pltpu.VMEM((3,) + velocity.shape, f32),
+            pltpu.VMEM((3, 3, layers, rows // PTS, PTS, PTS, cols), f32),
             pltpu.VMEM((4, planes, rows, cols), f32),
             pltpu.VMEM((2, 4, planes * rows), f32),
             pltpu.VMEM((2, 4, planes, cols), f32),
@@ -490,12 +598,15 @@
             pltpu.VMEM((len(YZOFF), 4, 1, cols), f32),
             pltpu.VMEM((2, cols), f32),
             pltpu.VMEM((count, 2, cols), f32),
+            pltpu.VMEM((2, cols), f32),
             pltpu.VMEM((2, 4, rows, cols), f32),
             pltpu.VMEM(mass_weights.shape, f32),
             pltpu.VMEM((16, planes * rows), f32),
-            pltpu.SemaphoreType.DMA((9,)),
+            pltpu.SemaphoreType.DMA((6 + 3 * layers,)),
             pltpu.SemaphoreType.DMA((len(OFFS),)),
             pltpu.SemaphoreType.DMA((len(OFFS),)),
+            pltpu.SemaphoreType.DMA,
+            pltpu.SemaphoreType.DMA((2,)),
             pltpu.SemaphoreType.DMA,
             pltpu.SemaphoreType.DMA,
             pltpu.SemaphoreType.DMA((len(FACES), 4)),

time: 14.7 us -> 13.8 us (0.939)
  the two profiles are of different devices: /device:TPU:0 before, /device:TPU:1 now
where the time goes in v1:
time: 13.8 us; the launch traced here: 13.7 us
  Pallas kernels  13 us (94%)
  between operations  0.64 us (5%)
    pallas_call x1, Pallas kernels, per_device(): pl.pallas_call(functools.partial(kernel, sizes), out_shape=(jax.ShapeDtyp...  12.1 us
    pallas_call x1, Pallas kernels, per_device(): pl.pallas_call(finish, out_shape=(jax.ShapeDtypeStruct(velocity.shape, f3...  0.95 us

profile of v1, /device:TPU:1, one launch (start us, length us, event | category | flops | bytes accessed | tf_op | source)
XLA Modules:
  0.0 13.7 jit_solution(11370126602496558602)
XLA Ops:
  0.6 12.1 %shard_map.112 = (f32[3,16,32,128]{3,2,1,0:T(8,128)S(1)}, f32[3,16,32,128]{3,2,1,0:T(8,128)S(1)}, f32[2,128]{1,0:T(2,128)S(1)}) custom-call(f32[3,16,32,128]{3,2,1,0:T(8,128)} %v_hbm.1, bf16[6,16,32,128]{3,2,1,0:T(8,128)(2,1)} %g_hbm.1, bf16[16,32,128]{2,1,0:T(8,128)(2,1)} %m_hbm.1, bf16[256,256]{1,0:T(8,128)(2,1)} %constant.12.clone.dx_hbm, ...), custom_call_target="tpu_custom_call" | custom-call | tf_op jit(solution)/shard_map/pallas_call | solution.py:576
  12.7 1.0 %shard_map.113 = (f32[3,16,32,128]{3,2,1,0:T(8,128)}, f32[1,1]{1,0:T(1,128)}, f32[1,1]{1,0:T(1,128)}) custom-call(f32[3,16,32,128]{3,2,1,0:T(8,128)S(1)} %get-tuple-element.9.a_ref, f32[3,16,32,128]{3,2,1,0:T(8,128)S(1)} %get-tuple-element.10.b_ref, f32[2,128]{1,0:T(2,128)S(1)} %get-tuple-element.11.s_ref), custom_call_target="tpu_custom_call" | custom-call | tf_op jit(solution)/shard_map/pallas_call | solution.py:620

commit v2 on v1

--- a/solution.py
+++ b/solution.py
@@ -54,17 +54,20 @@
 def tables(cols):
     d = gll_derivative(ORDER)
     eye = np.eye(PTS, dtype=np.float32)
-    out = []
-    for mat in (d, d.T):
+
+    def lanes(mat):
         hi, lo = split_np(np.kron(np.eye(cols // PTS, dtype=np.float32), mat.T))
-        zero = np.zeros_like(lo)
-        out.append(np.block([[hi, lo], [hi, zero]]))
-        hi, lo = split_np(np.concatenate([np.kron(eye, mat), np.kron(mat, eye)]))
-        out.append(np.concatenate([hi, hi, lo, lo], axis=1))
-    pick = np.zeros((2 * PTS, 2 * cols), np.float32)
-    pick[0, [0, cols]] = 1.0
-    pick[1, [cols - 1, 2 * cols - 1]] = 1.0
-    out.append(pick.astype(jnp.bfloat16))
+        return np.block([[hi, lo], [hi, np.zeros_like(lo)]])
+
+    def paired(mat):
+        hi, lo = split_np(mat)
+        zero = np.zeros_like(hi)
+        return np.concatenate([np.block([[t, t, zero, zero], [zero, zero, t, t]]) for t in (hi, lo)])
+
+    hi, lo = split_np(np.concatenate([np.kron(eye, d), np.kron(d, eye)]))
+    out = [lanes(d), np.concatenate([hi, hi, lo, lo], axis=1)]
+    out.append(lanes(d.T))
+    out.append(np.stack([paired(np.kron(eye, d.T)), paired(np.kron(d.T, eye))]))
     put = np.zeros((16, 4 * cols), np.float32)
     for c in range(4):
         for base in (0, 8):
@@ -90,6 +93,18 @@
     return r[:, :cols] + r[:, cols:]
 
 
+def tree(terms):
+    while len(terms) > 1:
+        odd = terms[len(terms) // 2 * 2:]
+        terms = [a + b for a, b in zip(terms[::2], terms[1::2])] + odd
+    return terms[0]
+
+
+def quad(pairs):
+    deep = [jnp.concatenate([*pairs[k], *pairs[k + 1]], axis=0) for k in (0, 2)]
+    return jnp.concatenate(deep, axis=1)
+
+
 def stacked(pairs):
     hi = jnp.concatenate([p[0] for p in pairs], axis=1)
     lo = jnp.concatenate([p[1] for p in pairs], axis=1)
@@ -98,9 +113,9 @@
 
 def kernel(
     sizes,
-    v_hbm, g_hbm, m_hbm, dx_hbm, dyz_hbm, tx_hbm, tyz_hbm, pick_hbm, put_hbm,
+    v_hbm, g_hbm, m_hbm, dx_hbm, dyz_hbm, tx_hbm, tyz_hbm, put_hbm,
     a_out, b_out, s_out,
-    v, g, m, dx_ref, dyz_ref, tx_ref, tyz_ref, pick_ref, put_ref, flux, field, pack, yface, yzrow, rpack, ryface, rzface, ryz, part, parts, low, zface, keep, halo,
+    v, g, m, dx_ref, dyz_ref, tx_ref, tyz_ref, put_ref, flux, field, ends, pack, yface, yzrow, rpack, ryface, rzface, ryz, part, parts, low, zface, keep, halo,
     in_sem, send_sem, recv_sem, ssend, srecv, lsend, lrecv, fsend, frecv,
 ):
     nx, ny, nz = sizes
@@ -120,17 +135,14 @@
             c.start()
         return cs
 
+    def load_layer(e):
+        at = pl.ds(e * PTS, PTS)
+        return start(
+            [(v_hbm.at[:, at], v.at[:, at]), (g_hbm.at[:, at], g.at[:, at]), (m_hbm.at[at], m.at[at])], 2 + 3 * e
+        )
+
+    loads = [load_layer(0)]
     tabs = start([(dx_hbm, dx_ref), (dyz_hbm, dyz_ref)], 0)
-    loads = []
-    for e in range(layers):
-        at = pl.ds(e * PTS, PTS)
-        k = 2 + 3 * e
-        loads.append(
-            start([(v_hbm.at[:, at], v.at[:, at]), (m_hbm.at[at], m.at[at]), (g_hbm.at[:, at], g.at[:, at])], k)
-        )
-    late_tabs = start(
-        [(tx_hbm, tx_ref), (tyz_hbm, tyz_ref), (pick_hbm, pick_ref), (put_hbm, put_ref)], 2 + 3 * layers
-    )
 
     def rank(x, y, z):
         return (y * nx + x) * nz + z
@@ -174,6 +186,8 @@
     @pl.when(is_up)
     def _():
         for_targets(lows, greet_low)
+
+    loads += [load_layer(e) for e in range(1, layers)]
 
     def cross(i, n):
         return 1 + jnp.where(i > 0, 1, 0) + jnp.where(i < n - 1, 1, 0)
@@ -218,6 +232,17 @@
         for y, t in enumerate(assemble_xy(blocks)):
             field[c, pl.ds(e * PTS, PTS), y * PTS:(y + 1) * PTS, :] = t
 
+    pair_of = lax.broadcasted_iota(jnp.int32, (rows, cols), 1) // 2
+
+    def pack_sides():
+        step = cols // rows
+        for k in range(planes // step):
+            t = ends[pl.ds(k * step, step)].reshape(cols, cols).T
+            for c in range(4):
+                for s in range(2):
+                    r = 2 * c + 1 - s
+                    pack[s, c:c + 1, k * cols:(k + 1) * cols] = t[r:r + 1]
+
     def finish_channel(c):
         for e in range(1, layers):
             low = field[c, e * PTS - 1]
@@ -225,14 +250,9 @@
             both = low + high
             field[c, e * PTS - 1] = both
             field[c, e * PTS] = both
-        for e in range(layers):
-            x = field[c, pl.ds(e * PTS, PTS)].reshape(n_rows, cols)
-            r = lax.dot_general(
-                pick_ref[...], jnp.concatenate(split(x), axis=1), (((1,), (1,)), ((), ())),
-                preferred_element_type=jnp.float32,
-            )
-            for s in range(2):
-                pack[s, pl.ds(c, 1), pl.ds(e * n_rows, n_rows)] = r[s:s + 1]
+        for k in range(planes):
+            t = pltpu.roll(field[c, k], 2 * c + 1, 1)
+            ends[k] = jnp.where(pair_of == c, t, 0.0 if c == 3 else ends[k])
         for side, y in ((0, 0), (1, rows - 1)):
             face = field[c, :, y, :]
             yface[side, c] = face
@@ -305,31 +325,30 @@
         if y == yel - 1:
             w = w * unit((k_at < ORDER) | (iy < ny - 1)).reshape(1, PTS, cols)
         keep[:, y * PTS:(y + 1) * PTS, :] = w * inner_z
-    for c in tabs:
-        c.wait()
-    zero = jnp.zeros((PTS, cols), jnp.float32)
-    kin, ens = zero, zero
     n_blk = PTS * PTS
+    tile = (PTS, PTS, cols)
+    kin, ens = [], []
     for e in range(layers):
-        for c in loads[e]:
+        for c in loads[e] + (tabs if e == 0 else []):
             c.wait()
+        if e == 0:
+            late_tabs = start(
+                [(tx_hbm, tx_ref), (tyz_hbm, tyz_ref), (put_hbm, put_ref)], 2 + 3 * layers
+            )
         at = pl.ds(e * PTS, PTS)
         mass = m[at].astype(jnp.float32)
         geo = [g[k, at].astype(jnp.float32) for k in range(6)]
         square = None
         for c in range(3):
             block = v[c, at]
-            sq = block * block
-            square = sq if square is None else square + sq
-            blks = [block[:, y * PTS:(y + 1) * PTS, :].reshape(n_blk, cols) for y in range(yel)]
-            pairs = [split(b) for b in blks]
+            square = block * block if square is None else square + block * block
+            pairs = [split(block[:, y * PTS:(y + 1) * PTS, :].reshape(n_blk, cols)) for y in range(yel)]
             whole = tuple(jnp.concatenate([p[s] for p in pairs], axis=0) for s in range(2))
             gr_all = along_x(whole, dx_ref[...])
             for y0 in range(0, yel, 2):
                 r = dot(dyz_ref[...], stacked(pairs[y0:y0 + 2]))
                 for s in range(2):
                     y = y0 + s
-                    tile = (PTS, PTS, cols)
                     gr = gr_all[y * n_blk:(y + 1) * n_blk].reshape(tile)
                     gs = r[:n_blk, s * cols:(s + 1) * cols].reshape(tile)
                     gt = r[n_blk:, s * cols:(s + 1) * cols].reshape(tile)
@@ -337,13 +356,13 @@
                     fr = g0 * gr + g3 * gs + g4 * gt
                     fs = g3 * gr + g1 * gs + g5 * gt
                     ft = g4 * gr + g5 * gs + g2 * gt
-                    ens = ens + jnp.sum(gr * fr + gs * fs + gt * ft, axis=0)
+                    ens.append(jnp.sum(gr * fr + gs * fs + gt * ft, axis=0))
                     flux[0, c, e, y] = fr
                     flux[1, c, e, y] = fs
                     flux[2, c, e, y] = ft
-        kin = kin + jnp.sum((mass * square).reshape(-1, PTS, cols), axis=0)
+        kin.append(jnp.sum((mass * square).reshape(-1, PTS, cols), axis=0))
     mine = jnp.concatenate(
-        [jnp.sum(kin, 0, keepdims=True) * 0.5, jnp.sum(ens, 0, keepdims=True)], axis=0
+        [jnp.sum(tree(kin), 0, keepdims=True) * 0.5, jnp.sum(tree(ens), 0, keepdims=True)], axis=0
     )
     part[...] = mine
 
@@ -370,9 +389,9 @@
     ahead = across + jnp.where(is_low, half - 1 - iy, ny - 1 - iy)
     turn = jnp.where((ix % 2 == 1) & (ix < nx - 1), 1, 0) + jnp.where(iz < nz - 1, 1, 0)
     ahead = jnp.where(iy == half - 1, jnp.maximum(ahead, 1 + turn), ahead)
-    slot = jnp.where(ahead <= 1, -1, jnp.where(ahead == 2, 0, 2))
-
-    @pl.when(slot < 0)
+    early = ahead <= 1
+
+    @pl.when(early)
     def _():
         meet()
     parts[me] = mine
@@ -384,21 +403,23 @@
         put_field(3, e, [x[:, y * PTS:(y + 1) * PTS, :].reshape(n_blk, cols) for y in range(yel)])
     finish_channel(3)
 
-    @pl.loop(0, 3)
-    def _(c):
+    for c in range(3):
         for e in range(layers):
             fr, fs, ft = ([split(flux[k, c, e, y].reshape(n_blk, cols)) for y in range(yel)] for k in range(3))
             whole = tuple(jnp.concatenate([p[s] for p in fr], axis=0) for s in range(2))
             x = along_x(whole, tx_ref[...])
-            blocks = []
-            for y0 in range(0, yel, 2):
-                r = dot(tyz_ref[0:n_blk], stacked(fs[y0:y0 + 2])) + dot(tyz_ref[n_blk:], stacked(ft[y0:y0 + 2]))
-                for s in range(2):
-                    y = y0 + s
-                    blocks.append(x[y * n_blk:(y + 1) * n_blk] + r[:, s * cols:(s + 1) * cols])
+            blocks = [x[y * n_blk:(y + 1) * n_blk] for y in range(yel)]
+            for y0 in range(0, yel, 4):
+                r = dot(tyz_ref[0], quad(fs[y0:y0 + 4])) + dot(tyz_ref[1], quad(ft[y0:y0 + 4]))
+                r = r[:2 * n_blk] + r[2 * n_blk:]
+                for s in range(4):
+                    deep = (s % 2) * n_blk
+                    blocks[y0 + s] += r[deep:deep + n_blk, (s // 2) * cols:(s // 2 + 1) * cols]
             put_field(c, e, blocks)
         finish_channel(c)
-        pl.when(slot == c)(meet)
+
+    pack_sides()
+    pl.when(jnp.logical_not(early))(meet)
 
     for off in OFFS:
         @pl.when(there(off))
@@ -408,11 +429,20 @@
     for c in range(4):
         send_faces(c)
 
-    def relay():
-        return pltpu.make_async_remote_copy(
-            src_ref=low, dst_ref=low, send_sem=lsend, recv_sem=lrecv,
-            device_id={"gx": ix, "gy": iy + 1, "gz": iz}, device_id_type=MESH,
-        )
+    odd = ix % 2 == 1
+
+    def relays():
+        return [
+            pltpu.make_async_remote_copy(
+                src_ref=low, dst_ref=low, send_sem=lsend.at[k], recv_sem=lrecv,
+                device_id={"gx": ix - k, "gy": iy + 1, "gz": iz}, device_id_type=MESH,
+            )
+            for k in range(2)
+        ]
+
+    def relay_on():
+        for c in relays():
+            c.start()
 
     def wait_rows(n, sem):
         rest = parts.at[pl.ds(0, n)]
@@ -425,15 +455,15 @@
     def low_wait():
         pltpu.make_async_copy(low, low, lrecv).wait()
 
-    @pl.when(iy == half - 1)
+    @pl.when((iy == half - 1) & odd)
     def _():
         low_sum()
-        relay().start()
-
-    @pl.when(is_up & (iy < ny - 1))
+        relay_on()
+
+    @pl.when(is_up & (iy < ny - 1) & odd)
     def _():
         low_wait()
-        relay().start()
+        relay_on()
 
     for off in OFFS:
         @pl.when(there(off))
@@ -515,7 +545,10 @@
     def _():
         wait_rows(n_low - 1, ssend)
 
-    @pl.when(is_low & (iy < half - 1))
+    sends_on = (iy >= half - 1) & (iy < ny - 1) & odd
+    later = jnp.logical_not(sends_on)
+
+    @pl.when(is_low & later)
     def _():
         low_sum()
 
@@ -523,13 +556,14 @@
     def _():
         wait_rows(count - 1, ssend)
 
-    @pl.when(iy == ny - 1)
+    @pl.when(is_up & later)
     def _():
         low_wait()
 
-    @pl.when((iy >= half - 1) & (iy < ny - 1))
-    def _():
-        relay().wait_send()
+    @pl.when(sends_on)
+    def _():
+        for c in relays():
+            c.wait_send()
 
     @pl.when(is_low)
     def _():
@@ -580,7 +614,7 @@
             jax.ShapeDtypeStruct(velocity.shape, f32),
             jax.ShapeDtypeStruct((2, cols), f32),
         ),
-        in_specs=[hbm] * 9,
+        in_specs=[hbm] * 8,
         out_specs=(vmem, vmem, vmem),
         scratch_shapes=[
             pltpu.VMEM(velocity.shape, f32),
@@ -589,6 +623,7 @@
             *[pltpu.VMEM(t.shape, t.dtype) for t in consts],
             pltpu.VMEM((3, 3, layers, rows // PTS, PTS, PTS, cols), f32),
             pltpu.VMEM((4, planes, rows, cols), f32),
+            pltpu.VMEM((planes, rows, cols), f32),
             pltpu.VMEM((2, 4, planes * rows), f32),
             pltpu.VMEM((2, 4, planes, cols), f32),
             pltpu.VMEM((2, 2, 4, 1, cols), f32),
@@ -602,12 +637,12 @@
             pltpu.VMEM((2, 4, rows, cols), f32),
             pltpu.VMEM(mass_weights.shape, f32),
             pltpu.VMEM((16, planes * rows), f32),
-            pltpu.SemaphoreType.DMA((6 + 3 * layers,)),
+            pltpu.SemaphoreType.DMA((5 + 3 * layers,)),
             pltpu.SemaphoreType.DMA((len(OFFS),)),
             pltpu.SemaphoreType.DMA((len(OFFS),)),
             pltpu.SemaphoreType.DMA,
             pltpu.SemaphoreType.DMA((2,)),
-            pltpu.SemaphoreType.DMA,
+            pltpu.SemaphoreType.DMA((2,)),
             pltpu.SemaphoreType.DMA,
             pltpu.SemaphoreType.DMA((len(FACES), 4)),
             pltpu.SemaphoreType.DMA((len(FACES), 4)),

time: 13.8 us -> 13.5 us (0.978)
  the two profiles are of different devices: /device:TPU:1 before, /device:TPU:0 now
where the time goes in v2:
time: 13.5 us; the launch traced here: 13.3 us
  Pallas kernels  12.7 us (94%)
  between operations  0.64 us (5%)
    pallas_call x1, Pallas kernels, per_device(): pl.pallas_call(functools.partial(kernel, sizes), out_shape=(jax.ShapeDtyp...  11.7 us
    pallas_call x1, Pallas kernels, per_device(): pl.pallas_call(finish, out_shape=(jax.ShapeDtypeStruct(velocity.shape, f3...  0.95 us

profile of v2, /device:TPU:0, one launch (start us, length us, event | category | flops | bytes accessed | tf_op | source)
XLA Modules:
  0.0 13.3 jit_solution(3959828317165455248)
XLA Ops:
  0.6 11.7 %shard_map.103 = (f32[3,16,32,128]{3,2,1,0:T(8,128)S(1)}, f32[3,16,32,128]{3,2,1,0:T(8,128)S(1)}, f32[2,128]{1,0:T(2,128)S(1)}) custom-call(f32[3,16,32,128]{3,2,1,0:T(8,128)} %v_hbm.1, bf16[6,16,32,128]{3,2,1,0:T(8,128)(2,1)} %g_hbm.1, bf16[16,32,128]{2,1,0:T(8,128)(2,1)} %m_hbm.1, bf16[256,256]{1,0:T(8,128)(2,1)} %constant.10.clone.dx_hbm, ...), custom_call_target="tpu_custom_call" | custom-call | tf_op jit(solution)/shard_map/pallas_call | solution.py:610
  12.4 1.0 %shard_map.104 = (f32[3,16,32,128]{3,2,1,0:T(8,128)}, f32[1,1]{1,0:T(1,128)}, f32[1,1]{1,0:T(1,128)}) custom-call(f32[3,16,32,128]{3,2,1,0:T(8,128)S(1)} %get-tuple-element.9.a_ref, f32[3,16,32,128]{3,2,1,0:T(8,128)S(1)} %get-tuple-element.10.b_ref, f32[2,128]{1,0:T(2,128)S(1)} %get-tuple-element.11.s_ref), custom_call_target="tpu_custom_call" | custom-call | tf_op jit(solution)/shard_map/pallas_call | solution.py:655

commit v3 on v2

--- a/solution.py
+++ b/solution.py
@@ -1,5 +1,6 @@
 import functools
 import itertools
+import math
 
 import jax
 import jax.numpy as jnp
@@ -11,6 +12,7 @@
 
 ORDER = 7
 PTS = ORDER + 1
+UNIT = 4 * 128 * 4
 MESH = pl.DeviceIdType.MESH
 AXES = ("gx", "gy", "gz")
 XOFF = [o for o in itertools.product((-1, 0, 1), repeat=3) if o[0] != 0]
@@ -115,8 +117,8 @@
     sizes,
     v_hbm, g_hbm, m_hbm, dx_hbm, dyz_hbm, tx_hbm, tyz_hbm, put_hbm,
     a_out, b_out, s_out,
-    v, g, m, dx_ref, dyz_ref, tx_ref, tyz_ref, put_ref, flux, field, ends, pack, yface, yzrow, rpack, ryface, rzface, ryz, part, parts, low, zface, keep, halo,
-    in_sem, send_sem, recv_sem, ssend, srecv, lsend, lrecv, fsend, frecv,
+    v, g, m, dx_ref, dyz_ref, tx_ref, tyz_ref, put_ref, flux, field, ends, pack, yface, yzrow, rpack, ryface, rzface, ryz, part, parts, low, units, zface, keep, halo,
+    in_sem, send_sem, recv_sem, ssend, srecv, lrecv,
 ):
     nx, ny, nz = sizes
     count = nx * ny * nz
@@ -129,20 +131,27 @@
     is_low = iy < half
     is_up = iy >= half
 
+    def span(*refs):
+        size = sum(math.prod(r.shape) * jnp.dtype(r.dtype).itemsize for r in refs)
+        assert size % UNIT == 0
+        return size // UNIT
+
+    def await_units(n, sem):
+        pltpu.make_async_copy(units.at[pl.ds(0, n)], units.at[pl.ds(0, n)], sem).wait()
+
     def start(pairs, k):
-        cs = [pltpu.make_async_copy(s, d, in_sem.at[k + i]) for i, (s, d) in enumerate(pairs)]
-        for c in cs:
-            c.start()
-        return cs
+        for src, dst in pairs:
+            pltpu.make_async_copy(src, dst, in_sem.at[k]).start()
+        return span(*(dst for _, dst in pairs))
 
     def load_layer(e):
         at = pl.ds(e * PTS, PTS)
         return start(
-            [(v_hbm.at[:, at], v.at[:, at]), (g_hbm.at[:, at], g.at[:, at]), (m_hbm.at[at], m.at[at])], 2 + 3 * e
+            [(v_hbm.at[:, at], v.at[:, at]), (g_hbm.at[:, at], g.at[:, at]), (m_hbm.at[at], m.at[at])], e
         )
 
     loads = [load_layer(0)]
-    tabs = start([(dx_hbm, dx_ref), (dyz_hbm, dyz_ref)], 0)
+    loads[0] += start([(dx_hbm, dx_ref), (dyz_hbm, dyz_ref)], 0)
 
     def rank(x, y, z):
         return (y * nx + x) * nz + z
@@ -297,16 +306,16 @@
         else:
             src = yzrow.at[side(off[1]), side(off[2])]
         return pltpu.make_async_remote_copy(
-            src_ref=src, dst_ref=landing(opp), send_sem=send_sem.at[OFFS.index(off)],
-            recv_sem=recv_sem.at[OFFS.index(opp)], device_id=target(off), device_id_type=MESH,
+            src_ref=src, dst_ref=landing(opp), send_sem=send_sem, recv_sem=recv_sem,
+            device_id=target(off), device_id_type=MESH,
         )
 
     def face_copy(off, c):
         k, opp = FACES.index(off), FACES.index(tuple(-o for o in off))
         src, dst = (yface, ryface) if off[1] else (zface, rzface)
         return pltpu.make_async_remote_copy(
-            src_ref=src.at[k % 2, c], dst_ref=dst.at[opp % 2, c], send_sem=fsend.at[k, c],
-            recv_sem=frecv.at[opp, c], device_id=target(off), device_id_type=MESH,
+            src_ref=src.at[k % 2, c], dst_ref=dst.at[opp % 2, c], send_sem=send_sem,
+            recv_sem=recv_sem, device_id=target(off), device_id_type=MESH,
         )
 
     def send_faces(c):
@@ -329,11 +338,10 @@
     tile = (PTS, PTS, cols)
     kin, ens = [], []
     for e in range(layers):
-        for c in loads[e] + (tabs if e == 0 else []):
-            c.wait()
+        await_units(loads[e], in_sem.at[e])
         if e == 0:
             late_tabs = start(
-                [(tx_hbm, tx_ref), (tyz_hbm, tyz_ref), (put_hbm, put_ref)], 2 + 3 * layers
+                [(tx_hbm, tx_ref), (tyz_hbm, tyz_ref), (put_hbm, put_ref)], layers
             )
         at = pl.ds(e * PTS, PTS)
         mass = m[at].astype(jnp.float32)
@@ -396,8 +404,7 @@
         meet()
     parts[me] = mine
 
-    for c in late_tabs:
-        c.wait()
+    await_units(late_tabs, in_sem.at[layers])
     for e in range(layers):
         x = m[pl.ds(e * PTS, PTS)].astype(jnp.float32)
         put_field(3, e, [x[:, y * PTS:(y + 1) * PTS, :].reshape(n_blk, cols) for y in range(yel)])
@@ -434,7 +441,7 @@
     def relays():
         return [
             pltpu.make_async_remote_copy(
-                src_ref=low, dst_ref=low, send_sem=lsend.at[k], recv_sem=lrecv,
+                src_ref=low, dst_ref=low, send_sem=ssend, recv_sem=lrecv,
                 device_id={"gx": ix - k, "gy": iy + 1, "gz": iz}, device_id_type=MESH,
             )
             for k in range(2)
@@ -465,18 +472,22 @@
         low_wait()
         relay_on()
 
-    for off in OFFS:
-        @pl.when(there(off))
-        def _(off=off):
-            dst = landing(off)
-            pltpu.make_async_copy(dst, dst, recv_sem.at[OFFS.index(off)]).wait()
-
-    for k, off in enumerate(FACES):
-        @pl.when(there(off))
-        def _(k=k, off=off):
-            for c in range(4):
-                dst = (ryface if off[1] else rzface).at[k % 2, c]
-                pltpu.make_async_copy(dst, dst, frecv.at[k, c]).wait()
+    def beside(i, n):
+        return jnp.where(i > 0, 1, 0) + jnp.where(i < n - 1, 1, 0)
+
+    bx, by, bz = (beside(i, n) for i, n in zip(here, sizes))
+    edge = span(landing((1, 0, 1)))
+    whole_x = span(landing((1, 0, 0)))
+    corner = span(landing((0, 1, 1)))
+    def await_neighbours(sem):
+        for x, y, z in itertools.product(*(((0,), (1,), (1, 2))[min(n, 3) - 1] for n in sizes)):
+            n = (
+                x * (1 + y) * (whole_x + z * edge) + y * z * corner
+                + y * span(ryface.at[0]) + z * span(rzface.at[0])
+            )
+            pl.when((bx == x) & (by == y) & (bz == z))(functools.partial(await_units, n, sem))
+
+    await_neighbours(recv_sem)
 
     pshape = (4, total_rows)
     place = lax.broadcasted_iota(jnp.int32, (1, total_rows), 1)
@@ -528,42 +539,23 @@
             a_out[c, at] = (field[c, at] + x[:, c * cols:(c + 1) * cols].reshape(PTS, rows, cols)) * w
             b_out[c, at] = mass * v[c, at]
 
-    for off in OFFS:
-        @pl.when(there(off))
-        def _(off=off):
-            copy_to(off).wait_send()
-
-    for off in FACES:
-        @pl.when(there(off))
-        def _(off=off):
-            for c in range(4):
-                face_copy(off, c).wait_send()
-
+    await_neighbours(send_sem)
     n_up = count - n_low
-
-    @pl.when(is_low)
-    def _():
-        wait_rows(n_low - 1, ssend)
 
     sends_on = (iy >= half - 1) & (iy < ny - 1) & odd
     later = jnp.logical_not(sends_on)
+    for low_one, relays_too in itertools.product((True, False), repeat=2):
+        n = (n_low - 1 if low_one else count - 1) + (2 if relays_too else 0)
+        ok = (is_low if low_one else is_up) & (sends_on if relays_too else later)
+        pl.when(ok)(functools.partial(wait_rows, n, ssend))
 
     @pl.when(is_low & later)
     def _():
         low_sum()
 
-    @pl.when(is_up)
-    def _():
-        wait_rows(count - 1, ssend)
-
     @pl.when(is_up & later)
     def _():
         low_wait()
-
-    @pl.when(sends_on)
-    def _():
-        for c in relays():
-            c.wait_send()
 
     @pl.when(is_low)
     def _():
@@ -585,18 +577,15 @@
     rayleigh = ens / (2.0 * kin)
     k[...] = kin[:, 0:1]
     e[...] = ens[:, 0:1]
-    outs = [
-        pltpu.make_async_copy(k, k_hbm, sem.at[chunks]),
-        pltpu.make_async_copy(e, e_hbm, sem.at[chunks + 1]),
-    ]
     for c in range(chunks):
         r[c] = a_ref[c] - rayleigh[None] * b_ref[c]
-        outs.append(pltpu.make_async_copy(r.at[c], r_hbm.at[c], sem.at[c]))
-        outs[-1].start()
-    outs[0].start()
-    outs[1].start()
+        pltpu.make_async_copy(r.at[c], r_hbm.at[c], sem.at[0]).start()
+    outs = [pltpu.make_async_copy(k, k_hbm, sem.at[1]), pltpu.make_async_copy(e, e_hbm, sem.at[2])]
+    for c in outs:
+        c.start()
     for c in outs:
         c.wait()
+    pltpu.make_async_copy(r, r_hbm, sem.at[0]).wait()
 
 
 def per_device(sizes, velocity, geometry, mass_weights):
@@ -632,20 +621,18 @@
             pltpu.VMEM((2, 4, rows, cols), f32),
             pltpu.VMEM((len(YZOFF), 4, 1, cols), f32),
             pltpu.VMEM((2, cols), f32),
-            pltpu.VMEM((count, 2, cols), f32),
+            pltpu.VMEM((count + 2, 2, cols), f32),
             pltpu.VMEM((2, cols), f32),
+            pltpu.VMEM((velocity.size * 8 // UNIT, 4, 128), f32),
             pltpu.VMEM((2, 4, rows, cols), f32),
             pltpu.VMEM(mass_weights.shape, f32),
             pltpu.VMEM((16, planes * rows), f32),
-            pltpu.SemaphoreType.DMA((5 + 3 * layers,)),
-            pltpu.SemaphoreType.DMA((len(OFFS),)),
-            pltpu.SemaphoreType.DMA((len(OFFS),)),
+            pltpu.SemaphoreType.DMA((layers + 1,)),
+            pltpu.SemaphoreType.DMA,
+            pltpu.SemaphoreType.DMA,
             pltpu.SemaphoreType.DMA,
             pltpu.SemaphoreType.DMA((2,)),
-            pltpu.SemaphoreType.DMA((2,)),
             pltpu.SemaphoreType.DMA,
-            pltpu.SemaphoreType.DMA((len(FACES), 4)),
-            pltpu.SemaphoreType.DMA((len(FACES), 4)),
         ],
         compiler_params=pltpu.CompilerParams(
             collective_id=0, has_side_effects=True, vmem_limit_bytes=32 * 1024 * 1024
@@ -661,7 +648,7 @@
             pltpu.VMEM(velocity.shape, f32),
             pltpu.VMEM((1, 1), f32),
             pltpu.VMEM((1, 1), f32),
-            pltpu.SemaphoreType.DMA((velocity.shape[0] + 2,)),
+            pltpu.SemaphoreType.DMA((3,)),
         ],
         compiler_params=pltpu.CompilerParams(vmem_limit_bytes=8 * 1024 * 1024),
     )(applied, weighted, scalars)

time: 13.5 us -> 12.7 us (0.941)
  Pallas kernels: 12.7 us -> 11.9 us
    pallas_call x1, Pallas kernels: 11.7 us -> 11 us  [per_device(): pl.pallas_call(functools.partial(kernel, sizes), out_shape=(jax.ShapeDtyp...]
where the time goes in v3:
time: 12.7 us; the launch traced here: 12.5 us
  Pallas kernels  11.9 us (94%)
  between operations  0.64 us (5%)
    pallas_call x1, Pallas kernels, per_device(): pl.pallas_call(functools.partial(kernel, sizes), out_shape=(jax.ShapeDtyp...  11 us
    pallas_call x1, Pallas kernels, per_device(): pl.pallas_call(finish, out_shape=(jax.ShapeDtypeStruct(velocity.shape, f3...  0.94 us

profile of v3, /device:TPU:0, one launch (start us, length us, event | category | flops | bytes accessed | tf_op | source)
XLA Modules:
  0.0 12.5 jit_solution(4849975076216230370)
XLA Ops:
  0.6 11.0 %shard_map.103 = (f32[3,16,32,128]{3,2,1,0:T(8,128)S(1)}, f32[3,16,32,128]{3,2,1,0:T(8,128)S(1)}, f32[2,128]{1,0:T(2,128)S(1)}) custom-call(f32[3,16,32,128]{3,2,1,0:T(8,128)} %v_hbm.1, bf16[6,16,32,128]{3,2,1,0:T(8,128)(2,1)} %g_hbm.1, bf16[16,32,128]{2,1,0:T(8,128)(2,1)} %m_hbm.1, bf16[256,256]{1,0:T(8,128)(2,1)} %constant.10.clone.dx_hbm, ...), custom_call_target="tpu_custom_call" | custom-call | tf_op jit(solution)/shard_map/pallas_call | solution.py:599
  11.6 0.9 %shard_map.104 = (f32[3,16,32,128]{3,2,1,0:T(8,128)}, f32[1,1]{1,0:T(1,128)}, f32[1,1]{1,0:T(1,128)}) custom-call(f32[3,16,32,128]{3,2,1,0:T(8,128)S(1)} %get-tuple-element.9.a_ref, f32[3,16,32,128]{3,2,1,0:T(8,128)S(1)} %get-tuple-element.10.b_ref, f32[2,128]{1,0:T(2,128)S(1)} %get-tuple-element.11.s_ref), custom_call_target="tpu_custom_call" | custom-call | tf_op jit(solution)/shard_map/pallas_call | solution.py:642

commit v4 on v3

--- a/solution.py
+++ b/solution.py
@@ -117,7 +117,7 @@
     sizes,
     v_hbm, g_hbm, m_hbm, dx_hbm, dyz_hbm, tx_hbm, tyz_hbm, put_hbm,
     a_out, b_out, s_out,
-    v, g, m, dx_ref, dyz_ref, tx_ref, tyz_ref, put_ref, flux, field, ends, pack, yface, yzrow, rpack, ryface, rzface, ryz, part, parts, low, units, zface, keep, halo,
+    v, g, m, dx_ref, dyz_ref, tx_ref, tyz_ref, put_ref, grad, field, ends, pack, yface, yzrow, rpack, ryface, rzface, ryz, part, parts, low, units, zface, keep, halo,
     in_sem, send_sem, recv_sem, ssend, srecv, lrecv,
 ):
     nx, ny, nz = sizes
@@ -147,9 +147,10 @@
     def load_layer(e):
         at = pl.ds(e * PTS, PTS)
         return start(
-            [(v_hbm.at[:, at], v.at[:, at]), (g_hbm.at[:, at], g.at[:, at]), (m_hbm.at[at], m.at[at])], e
+            [(v_hbm.at[:, at], v.at[:, at]), (g_hbm.at[:, at], g.at[:, at])], e
         )
 
+    mass_load = start([(m_hbm, m)], layers + 1)
     loads = [load_layer(0)]
     loads[0] += start([(dx_hbm, dx_ref), (dyz_hbm, dyz_ref)], 0)
 
@@ -220,13 +221,14 @@
 
     def assemble_xy(blocks):
         tiles = (PTS, PTS, cols)
-        lane_next, lane_prev = x_next.reshape(1, PTS, cols), x_prev.reshape(1, PTS, cols)
+        lane_joint = (x_next + x_prev).reshape(1, PTS, cols)
+        at_last = jnp.broadcast_to((lane % PTS == ORDER).reshape(1, PTS, cols), tiles)
         last, first = y_last.reshape(1, PTS, cols), y_first.reshape(1, PTS, cols)
         xs = []
         for x in blocks:
             up = pltpu.roll(x, cols - 1, 1).reshape(tiles)
             down = pltpu.roll(x, 1, 1).reshape(tiles)
-            xs.append(x.reshape(tiles) + up * lane_next + down * lane_prev)
+            xs.append(x.reshape(tiles) + jnp.where(at_last, up, down) * lane_joint)
         out = []
         for y in range(yel):
             t = xs[y]
@@ -336,6 +338,12 @@
         keep[:, y * PTS:(y + 1) * PTS, :] = w * inner_z
     n_blk = PTS * PTS
     tile = (PTS, PTS, cols)
+    await_units(mass_load, in_sem.at[layers + 1])
+    for e in range(layers):
+        x = m[pl.ds(e * PTS, PTS)].astype(jnp.float32)
+        put_field(3, e, [x[:, y * PTS:(y + 1) * PTS, :].reshape(n_blk, cols) for y in range(yel)])
+    finish_channel(3)
+
     kin, ens = [], []
     for e in range(layers):
         await_units(loads[e], in_sem.at[e])
@@ -345,7 +353,8 @@
             )
         at = pl.ds(e * PTS, PTS)
         mass = m[at].astype(jnp.float32)
-        geo = [g[k, at].astype(jnp.float32) for k in range(6)]
+        geo = [g[k, at].astype(jnp.float32) for k in range(3)]
+        geo += [(g[k, at] + g[k, at]).astype(jnp.float32) for k in range(3, 6)]
         square = None
         for c in range(3):
             block = v[c, at]
@@ -360,14 +369,12 @@
                     gr = gr_all[y * n_blk:(y + 1) * n_blk].reshape(tile)
                     gs = r[:n_blk, s * cols:(s + 1) * cols].reshape(tile)
                     gt = r[n_blk:, s * cols:(s + 1) * cols].reshape(tile)
-                    g0, g1, g2, g3, g4, g5 = (t[:, y * PTS:(y + 1) * PTS, :] for t in geo)
-                    fr = g0 * gr + g3 * gs + g4 * gt
-                    fs = g3 * gr + g1 * gs + g5 * gt
-                    ft = g4 * gr + g5 * gs + g2 * gt
-                    ens.append(jnp.sum(gr * fr + gs * fs + gt * ft, axis=0))
-                    flux[0, c, e, y] = fr
-                    flux[1, c, e, y] = fs
-                    flux[2, c, e, y] = ft
+                    g0, g1, g2, g33, g44, g55 = (t[:, y * PTS:(y + 1) * PTS, :] for t in geo)
+                    form = gr * (g0 * gr + g33 * gs + g44 * gt) + gs * (g1 * gs + g55 * gt) + gt * (g2 * gt)
+                    ens.append(jnp.sum(form, axis=0))
+                    grad[0, c, e, y] = gr
+                    grad[1, c, e, y] = gs
+                    grad[2, c, e, y] = gt
         kin.append(jnp.sum((mass * square).reshape(-1, PTS, cols), axis=0))
     mine = jnp.concatenate(
         [jnp.sum(tree(kin), 0, keepdims=True) * 0.5, jnp.sum(tree(ens), 0, keepdims=True)], axis=0
@@ -405,14 +412,23 @@
     parts[me] = mine
 
     await_units(late_tabs, in_sem.at[layers])
-    for e in range(layers):
-        x = m[pl.ds(e * PTS, PTS)].astype(jnp.float32)
-        put_field(3, e, [x[:, y * PTS:(y + 1) * PTS, :].reshape(n_blk, cols) for y in range(yel)])
-    finish_channel(3)
+
+    metric = {
+        (e, y): [g[k, pl.ds(e * PTS, PTS), pl.ds(y * PTS, PTS)].astype(jnp.float32) for k in range(6)]
+        for e in range(layers) for y in range(yel)
+    }
+
+    def fluxes(c, e, y):
+        g0, g1, g2, g3, g4, g5 = metric[e, y]
+        gr, gs, gt = (grad[k, c, e, y] for k in range(3))
+        return g0 * gr + g3 * gs + g4 * gt, g3 * gr + g1 * gs + g5 * gt, g4 * gr + g5 * gs + g2 * gt
 
     for c in range(3):
         for e in range(layers):
-            fr, fs, ft = ([split(flux[k, c, e, y].reshape(n_blk, cols)) for y in range(yel)] for k in range(3))
+            fr, fs, ft = [], [], []
+            for y in range(yel):
+                for store, f in zip((fr, fs, ft), fluxes(c, e, y)):
+                    store.append(split(f.reshape(n_blk, cols)))
             whole = tuple(jnp.concatenate([p[s] for p in fr], axis=0) for s in range(2))
             x = along_x(whole, tx_ref[...])
             blocks = [x[y * n_blk:(y + 1) * n_blk] for y in range(yel)]
@@ -627,7 +643,7 @@
             pltpu.VMEM((2, 4, rows, cols), f32),
             pltpu.VMEM(mass_weights.shape, f32),
             pltpu.VMEM((16, planes * rows), f32),
-            pltpu.SemaphoreType.DMA((layers + 1,)),
+            pltpu.SemaphoreType.DMA((layers + 2,)),
             pltpu.SemaphoreType.DMA,
             pltpu.SemaphoreType.DMA,
             pltpu.SemaphoreType.DMA,

time: 12.7 us -> 12.6 us (level)
    pallas_call x1, Pallas kernels: 11 us -> 10.8 us  [per_device(): pl.pallas_call(functools.partial(kernel, sizes), out_shape=(jax.ShapeDtyp...]
where the time goes in v4:
time: 12.6 us; the launch traced here: 12.4 us
  Pallas kernels  11.8 us (94%)
  between operations  0.64 us (5%)
    pallas_call x1, Pallas kernels, per_device(): pl.pallas_call(functools.partial(kernel, sizes), out_shape=(jax.ShapeDtyp...  10.8 us
    pallas_call x1, Pallas kernels, per_device(): pl.pallas_call(finish, out_shape=(jax.ShapeDtypeStruct(velocity.shape, f3...  0.94 us

profile of v4, /device:TPU:0, one launch (start us, length us, event | category | flops | bytes accessed | tf_op | source)
XLA Modules:
  0.0 12.4 jit_solution(2018102076606725817)
XLA Ops:
  0.6 10.8 %shard_map.103 = (f32[3,16,32,128]{3,2,1,0:T(8,128)S(1)}, f32[3,16,32,128]{3,2,1,0:T(8,128)S(1)}, f32[2,128]{1,0:T(2,128)S(1)}) custom-call(f32[3,16,32,128]{3,2,1,0:T(8,128)} %v_hbm.1, bf16[6,16,32,128]{3,2,1,0:T(8,128)(2,1)} %g_hbm.1, bf16[16,32,128]{2,1,0:T(8,128)(2,1)} %m_hbm.1, bf16[256,256]{1,0:T(8,128)(2,1)} %constant.10.clone.dx_hbm, ...), custom_call_target="tpu_custom_call" | custom-call | tf_op jit(solution)/shard_map/pallas_call | solution.py:615
  11.5 0.9 %shard_map.104 = (f32[3,16,32,128]{3,2,1,0:T(8,128)}, f32[1,1]{1,0:T(1,128)}, f32[1,1]{1,0:T(1,128)}) custom-call(f32[3,16,32,128]{3,2,1,0:T(8,128)S(1)} %get-tuple-element.9.a_ref, f32[3,16,32,128]{3,2,1,0:T(8,128)S(1)} %get-tuple-element.10.b_ref, f32[2,128]{1,0:T(2,128)S(1)} %get-tuple-element.11.s_ref), custom_call_target="tpu_custom_call" | custom-call | tf_op jit(solution)/shard_map/pallas_call | solution.py:658

commit v5 on v4

--- a/solution.py
+++ b/solution.py
@@ -118,7 +118,7 @@
     v_hbm, g_hbm, m_hbm, dx_hbm, dyz_hbm, tx_hbm, tyz_hbm, put_hbm,
     a_out, b_out, s_out,
     v, g, m, dx_ref, dyz_ref, tx_ref, tyz_ref, put_ref, grad, field, ends, pack, yface, yzrow, rpack, ryface, rzface, ryz, part, parts, low, units, zface, keep, halo,
-    in_sem, send_sem, recv_sem, ssend, srecv, lrecv,
+    in_sem, send_sem, recv_sem, ssend, srecv,
 ):
     nx, ny, nz = sizes
     count = nx * ny * nz
@@ -150,7 +150,7 @@
             [(v_hbm.at[:, at], v.at[:, at]), (g_hbm.at[:, at], g.at[:, at])], e
         )
 
-    mass_load = start([(m_hbm, m)], layers + 1)
+    mass_load = start([(m_hbm, m)], layers)
     loads = [load_layer(0)]
     loads[0] += start([(dx_hbm, dx_ref), (dyz_hbm, dyz_ref)], 0)
 
@@ -338,18 +338,28 @@
         keep[:, y * PTS:(y + 1) * PTS, :] = w * inner_z
     n_blk = PTS * PTS
     tile = (PTS, PTS, cols)
-    await_units(mass_load, in_sem.at[layers + 1])
-    for e in range(layers):
-        x = m[pl.ds(e * PTS, PTS)].astype(jnp.float32)
-        put_field(3, e, [x[:, y * PTS:(y + 1) * PTS, :].reshape(n_blk, cols) for y in range(yel)])
-    finish_channel(3)
+    across = (nx - 1) // 2 - ix // 2 + (nz - 1 - iz)
+    ahead = across + jnp.where(is_low, half - 1 - iy, ny - 1 - iy)
+    turn = jnp.where((ix % 2 == 1) & (ix < nx - 1), 1, 0) + jnp.where(iz < nz - 1, 1, 0)
+    ahead = jnp.where(iy == half - 1, jnp.maximum(ahead, 1 + turn), ahead)
+    early = ahead <= 1
+    last_to_start = early & is_up
+
+    def assemble_mass():
+        for e in range(layers):
+            x = m[pl.ds(e * PTS, PTS)].astype(jnp.float32)
+            put_field(3, e, [x[:, y * PTS:(y + 1) * PTS, :].reshape(n_blk, cols) for y in range(yel)])
+        finish_channel(3)
+
+    await_units(mass_load, in_sem.at[layers])
+    pl.when(jnp.logical_not(last_to_start))(assemble_mass)
 
     kin, ens = [], []
     for e in range(layers):
         await_units(loads[e], in_sem.at[e])
         if e == 0:
             late_tabs = start(
-                [(tx_hbm, tx_ref), (tyz_hbm, tyz_ref), (put_hbm, put_ref)], layers
+                [(tx_hbm, tx_ref), (tyz_hbm, tyz_ref), (put_hbm, put_ref)], 0
             )
         at = pl.ds(e * PTS, PTS)
         mass = m[at].astype(jnp.float32)
@@ -400,18 +410,13 @@
         def _():
             for_targets(ups, tell)
 
-    across = (nx - 1) // 2 - ix // 2 + (nz - 1 - iz)
-    ahead = across + jnp.where(is_low, half - 1 - iy, ny - 1 - iy)
-    turn = jnp.where((ix % 2 == 1) & (ix < nx - 1), 1, 0) + jnp.where(iz < nz - 1, 1, 0)
-    ahead = jnp.where(iy == half - 1, jnp.maximum(ahead, 1 + turn), ahead)
-    early = ahead <= 1
-
     @pl.when(early)
     def _():
         meet()
     parts[me] = mine
-
-    await_units(late_tabs, in_sem.at[layers])
+    pl.when(last_to_start)(assemble_mass)
+
+    await_units(late_tabs, in_sem.at[0])
 
     metric = {
         (e, y): [g[k, pl.ds(e * PTS, PTS), pl.ds(y * PTS, PTS)].astype(jnp.float32) for k in range(6)]
@@ -457,7 +462,7 @@
     def relays():
         return [
             pltpu.make_async_remote_copy(
-                src_ref=low, dst_ref=low, send_sem=ssend, recv_sem=lrecv,
+                src_ref=low, dst_ref=low, send_sem=ssend, recv_sem=srecv.at[0],
                 device_id={"gx": ix - k, "gy": iy + 1, "gz": iz}, device_id_type=MESH,
             )
             for k in range(2)
@@ -476,7 +481,7 @@
         low[...] = jnp.sum(parts[0:n_low], axis=0)
 
     def low_wait():
-        pltpu.make_async_copy(low, low, lrecv).wait()
+        pltpu.make_async_copy(low, low, srecv.at[0]).wait()
 
     @pl.when((iy == half - 1) & odd)
     def _():
@@ -643,12 +648,11 @@
             pltpu.VMEM((2, 4, rows, cols), f32),
             pltpu.VMEM(mass_weights.shape, f32),
             pltpu.VMEM((16, planes * rows), f32),
-            pltpu.SemaphoreType.DMA((layers + 2,)),
+            pltpu.SemaphoreType.DMA((layers + 1,)),
             pltpu.SemaphoreType.DMA,
             pltpu.SemaphoreType.DMA,
             pltpu.SemaphoreType.DMA,
             pltpu.SemaphoreType.DMA((2,)),
-            pltpu.SemaphoreType.DMA,
         ],
         compiler_params=pltpu.CompilerParams(
             collective_id=0, has_side_effects=True, vmem_limit_bytes=32 * 1024 * 1024

time: 12.6 us -> 12.5 us (level)
  no operation moved by 1% of the time
where the time goes in v5:
time: 12.5 us; the launch traced here: 12.4 us
  Pallas kernels  11.7 us (94%)
  between operations  0.64 us (5%)
    pallas_call x1, Pallas kernels, per_device(): pl.pallas_call(functools.partial(kernel, sizes), out_shape=(jax.ShapeDtyp...  10.8 us
    pallas_call x1, Pallas kernels, per_device(): pl.pallas_call(finish, out_shape=(jax.ShapeDtypeStruct(velocity.shape, f3...  0.94 us

profile of v5, /device:TPU:0, one launch (start us, length us, event | category | flops | bytes accessed | tf_op | source)
XLA Modules:
  0.0 12.4 jit_solution(2645023431663161036)
XLA Ops:
  0.6 10.8 %shard_map.103 = (f32[3,16,32,128]{3,2,1,0:T(8,128)S(1)}, f32[3,16,32,128]{3,2,1,0:T(8,128)S(1)}, f32[2,128]{1,0:T(2,128)S(1)}) custom-call(f32[3,16,32,128]{3,2,1,0:T(8,128)} %v_hbm.1, bf16[6,16,32,128]{3,2,1,0:T(8,128)(2,1)} %g_hbm.1, bf16[16,32,128]{2,1,0:T(8,128)(2,1)} %m_hbm.1, bf16[256,256]{1,0:T(8,128)(2,1)} %constant.10.clone.dx_hbm, ...), custom_call_target="tpu_custom_call" | custom-call | tf_op jit(solution)/shard_map/pallas_call | solution.py:620
  11.4 0.9 %shard_map.104 = (f32[3,16,32,128]{3,2,1,0:T(8,128)}, f32[1,1]{1,0:T(1,128)}, f32[1,1]{1,0:T(1,128)}) custom-call(f32[3,16,32,128]{3,2,1,0:T(8,128)S(1)} %get-tuple-element.9.a_ref, f32[3,16,32,128]{3,2,1,0:T(8,128)S(1)} %get-tuple-element.10.b_ref, f32[2,128]{1,0:T(2,128)S(1)} %get-tuple-element.11.s_ref), custom_call_target="tpu_custom_call" | custom-call | tf_op jit(solution)/shard_map/pallas_call | solution.py:662

commit v6 on v5

--- a/solution.py
+++ b/solution.py
@@ -224,6 +224,8 @@
         lane_joint = (x_next + x_prev).reshape(1, PTS, cols)
         at_last = jnp.broadcast_to((lane % PTS == ORDER).reshape(1, PTS, cols), tiles)
         last, first = y_last.reshape(1, PTS, cols), y_first.reshape(1, PTS, cols)
+        joint = first + last
+        in_last = jnp.broadcast_to((k_at == ORDER).reshape(1, PTS, cols), tiles)
         xs = []
         for x in blocks:
             up = pltpu.roll(x, cols - 1, 1).reshape(tiles)
@@ -232,10 +234,12 @@
         out = []
         for y in range(yel):
             t = xs[y]
-            if y < yel - 1:
-                t = t + pltpu.roll(xs[y + 1], PTS - 1, 1) * last
-            if y > 0:
-                t = t + pltpu.roll(xs[y - 1], 1, 1) * first
+            after = pltpu.roll(xs[y + 1], PTS - 1, 1) if y < yel - 1 else None
+            before = pltpu.roll(xs[y - 1], 1, 1) if y > 0 else None
+            if before is None or after is None:
+                t = t + (before * first if after is None else after * last)
+            else:
+                t = t + jnp.where(in_last, after, before) * joint
             out.append(t)
         return out
 

time: 12.5 us -> 12.5 us (level)
  no operation moved by 1% of the time
where the time goes in v6:
time: 12.5 us; the launch traced here: 12.4 us
  Pallas kernels  11.7 us (94%)
  between operations  0.64 us (5%)
    pallas_call x1, Pallas kernels, per_device(): pl.pallas_call(functools.partial(kernel, sizes), out_shape=(jax.ShapeDtyp...  10.8 us
    pallas_call x1, Pallas kernels, per_device(): pl.pallas_call(finish, out_shape=(jax.ShapeDtypeStruct(velocity.shape, f3...  0.94 us

profile of v6, /device:TPU:0, one launch (start us, length us, event | category | flops | bytes accessed | tf_op | source)
XLA Modules:
  0.0 12.4 jit_solution(174283090055670190)
XLA Ops:
  0.6 10.8 %shard_map.103 = (f32[3,16,32,128]{3,2,1,0:T(8,128)S(1)}, f32[3,16,32,128]{3,2,1,0:T(8,128)S(1)}, f32[2,128]{1,0:T(2,128)S(1)}) custom-call(f32[3,16,32,128]{3,2,1,0:T(8,128)} %v_hbm.1, bf16[6,16,32,128]{3,2,1,0:T(8,128)(2,1)} %g_hbm.1, bf16[16,32,128]{2,1,0:T(8,128)(2,1)} %m_hbm.1, bf16[256,256]{1,0:T(8,128)(2,1)} %constant.10.clone.dx_hbm, ...), custom_call_target="tpu_custom_call" | custom-call | tf_op jit(solution)/shard_map/pallas_call | solution.py:624
  11.4 0.9 %shard_map.104 = (f32[3,16,32,128]{3,2,1,0:T(8,128)}, f32[1,1]{1,0:T(1,128)}, f32[1,1]{1,0:T(1,128)}) custom-call(f32[3,16,32,128]{3,2,1,0:T(8,128)S(1)} %get-tuple-element.9.a_ref, f32[3,16,32,128]{3,2,1,0:T(8,128)S(1)} %get-tuple-element.10.b_ref, f32[2,128]{1,0:T(2,128)S(1)} %get-tuple-element.11.s_ref), custom_call_target="tpu_custom_call" | custom-call | tf_op jit(solution)/shard_map/pallas_call | solution.py:666
